TPU v7x, 32 devices: a whole 2x2x4 slice. The times are simulated.
32 devices in a mesh: rep: 1, dp: 32 (over x, y, z, core).
Axes of the slice: x: 2, y: 2, z: 4, core: 2. Of those that a mesh axis runs over, the one named last changes fastest.
Arguments:
- x: bfloat16 [32, 2048, 1024], P(('rep', 'dp'))
- dy: bfloat16 [32, 2048, 1024], P(('rep', 'dp'))
- w_gate: bfloat16 [2, 1024, 3200], replicated
- w_up: bfloat16 [2, 1024, 3200], replicated
- w_down: bfloat16 [2, 3200, 1024], replicated
- m_w_gate: float32 [2, 1024, 3200], P(None, 'dp')
- m_w_up: float32 [2, 1024, 3200], P(None, 'dp')
- m_w_down: float32 [2, 3200, 1024], P(None, 'dp')
- v_w_gate: float32 [2, 1024, 3200], P(None, 'dp')
- v_w_up: float32 [2, 1024, 3200], P(None, 'dp')
- v_w_down: float32 [2, 3200, 1024], P(None, 'dp')
Outputs:
- output 1: bfloat16 [2, 1024, 3200], P('rep')
- output 2: bfloat16 [2, 1024, 3200], P('rep')
- output 3: bfloat16 [2, 3200, 1024], P('rep')
- output 4: float32 [2, 1024, 3200], P('rep', 'dp')
- output 5: float32 [2, 1024, 3200], P('rep', 'dp')
- output 6: float32 [2, 3200, 1024], P('rep', 'dp')
- output 7: float32 [2, 1024, 3200], P('rep', 'dp')
- output 8: float32 [2, 1024, 3200], P('rep', 'dp')
- output 9: float32 [2, 3200, 1024], P('rep', 'dp')
All inputs are finite; a program needn't handle non-finite values.
Results may differ from a plain program's by a relative error of at most 0.022.
Values are sent between devices in bfloat16 or wider.
A program may use at most 2 GiB of HBM per device.

v0:
```python
import jax
import jax.numpy as jnp
from jax import lax

NAMES = ("w_gate", "w_up", "w_down")


def matmul(a, w):
    return jnp.dot(a, w, preferred_element_type=jnp.float32).astype(jnp.bfloat16)


def normed(h):
    wide = h.astype(jnp.float32)
    scale = lax.rsqrt(jnp.mean(wide**2, -1, keepdims=True) + 1e-6)
    return (wide * scale).astype(jnp.bfloat16)


def layer(h, w):
    a = normed(h)
    gate = jnp.dot(a, w["w_gate"], preferred_element_type=jnp.float32)
    up = jnp.dot(a, w["w_up"], preferred_element_type=jnp.float32)
    return h + matmul((jax.nn.silu(gate) * up).astype(jnp.bfloat16), w["w_down"])


def adamw(w, m, v, g):
    m = 0.9 * m + 0.1 * g
    v = 0.95 * v + 0.05 * g * g
    step = m * lax.rsqrt(v + 1e-8) + 0.1 * w
    return (w - 0.02 * step).astype(jnp.bfloat16), m, v


def stack(weights, h):
    for number in range(weights["w_gate"].shape[0]):
        h = layer(h, {name: w[number] for name, w in weights.items()})
    return h


def solution(mesh):
    groups = mesh.shape["rep"]

    def step(x, dy, *arrays):
        weights, m, v = (arrays[i : i + 3] for i in (0, 3, 6))
        x, dy = (t.reshape(groups, -1, *t.shape[1:]) for t in (x, dy))

        def of_a_group(x, dy):
            _, back = jax.vjp(lambda w: stack(w, x), dict(zip(NAMES, weights, strict=True)))
            by_weights = back(dy)[0]
            gradients = [by_weights[name].astype(jnp.float32) for name in NAMES]
            new = [adamw(w.astype(jnp.float32), m, v, g) for w, m, v, g in zip(weights, m, v, gradients, strict=True)]
            return tuple(one[which] for which in range(3) for one in new)

        return tuple(t.reshape(-1, *t.shape[2:]) for t in jax.vmap(of_a_group)(x, dy))

    return step
```

profile of v0, /device:TPU:0, one launch (start us, length us, event | category | flops | bytes accessed | tf_op | source)
XLA Modules:
  0.0 2024.5 jit_solution(1050835542886672453)
XLA Ops:
  20.1 22.3 %fusion.173 = f32[2048,3200]{1,0:T(8,128)} fusion(bf16[2,1024,3200]{2,1,0:T(8,128)(2,1)} %param.12, bf16[1,2048,1024]{1,2,0:T(8,128)(2,1)S(1)} %fusion.157), kind=kOutput, calls=%fused_computation.225 | convolution fusion | flops 13421772800 | bytes 36962304 | tf_op jit(solution)/vmap(jvp())/dot_general | solution.py:20
  42.3 30.0 %fusion.150 = (bf16[1,2048,3200]{2,1,0:T(8,128)(2,1)}, f32[2048,3200]{1,0:T(8,128)}) fusion(f32[2048,3200]{1,0:T(8,128)} %fusion.173, bf16[2,1024,3200]{2,1,0:T(8,128)(2,1)} %param.17, bf16[1,2048,1024]{1,2,0:T(8,128)(2,1)S(1)} %fusion.157), kind=kOutput, calls=%fused_computation.189 | convolution fusion | flops 13461094400 | bytes 76283904 | tf_op jit(solution)/vmap(jvp())/dot_general | solution.py:21
  72.3 22.1 %fusion.160 = (f32[2048]{0:T(1024)S(1)}, bf16[1,2048,1024]{1,2,0:T(8,128)(2,1)}) fusion(bf16[1,2048,1024]{1,2,0:T(8,128)(2,1)} %copy.18, bf16[2,3200,1024]{2,1,0:T(8,128)(2,1)} %param.15, bf16[1,2048,3200]{2,1,0:T(8,128)(2,1)} %get-tuple-element.301), kind=kOutput, calls=%fused_computation.212 | convolution fusion | flops 13432256512 | bytes 28057600 | tf_op jit(solution)/vmap(jvp())/dot_general | solution.py:9
  98.4 22.2 %fusion.163 = f32[2048,3200]{1,0:T(8,128)} fusion(bf16[2,1024,3200]{2,1,0:T(8,128)(2,1)} %param.12, bf16[1,2048,1024]{1,2,0:T(8,128)(2,1)S(1)} %fusion.161), kind=kOutput, calls=%fused_computation.215 | convolution fusion | flops 13421772800 | bytes 36962304 | tf_op jit(solution)/vmap(jvp())/dot_general | solution.py:20
  120.6 30.0 %fusion.149 = (bf16[1,2048,3200]{2,1,0:T(8,128)(2,1)}, f32[2048,3200]{1,0:T(8,128)}) fusion(f32[2048,3200]{1,0:T(8,128)} %fusion.163, bf16[2,1024,3200]{2,1,0:T(8,128)(2,1)} %param.17, bf16[1,2048,1024]{1,2,0:T(8,128)(2,1)S(1)} %fusion.161), kind=kOutput, calls=%fused_computation.187 | convolution fusion | flops 13461094400 | bytes 76283904 | tf_op jit(solution)/vmap(jvp())/dot_general | solution.py:21
  150.6 39.3 %convert_multiply_fusion.2 = (bf16[1,2048,3200]{2,1,0:T(8,128)(2,1)}, bf16[1,2048,3200]{2,1,0:T(8,128)(2,1)}) fusion(f32[2048,3200]{1,0:T(8,128)} %fusion.163, f32[2048,3200]{1,0:T(8,128)} %get-tuple-element.308, bf16[2,3200,1024]{2,1,0:T(8,128)(2,1)} %param.15, bf16[1,2048,1024]{2,1,0:T(8,128)(2,1)} %param.14), kind=kOutput, calls=%fused_computation.170 | convolution fusion | flops 13526630400 | bytes 89391104 | tf_op jit(solution)/vmap(transpose(jvp()))/dot_general | solution.py:9
  189.9 240.9 %while.14 = (bf16[1,2048,3200]{2,1,0:T(8,128)(2,1)}, bf16[1,2048,1024]{1,2,0:T(8,128)(2,1)}, f32[3200,32]{0,1:T(8,128)S(1)}, f32[3200,32]{0,1:T(8,128)}, u32[]{:...) while((bf16[1,2048,3200]{2,1,0:T(8,128)(2,1)}, ...), condition=%wide.windowed_dot_general_cond_rs.2.clone, body=%wide.windowed_dot_general_body_rs.2.clone.sunk | while | flops 1679384576 | bytes 49349200 | solution.py:21
  209.3 7.2 fusion.303
  255.6 7.2 fusion.301
  269.2 7.2 fusion.303
  299.5 7.2 fusion.303
  329.8 7.2 fusion.303
  376.7 7.2 fusion.301
  390.4 7.2 fusion.303
  437.5 19.9 fusion.142
  457.4 21.5 %fusion.162 = (f32[2048]{0:T(1024)S(1)}, bf16[2048,1024]{0,1:T(8,128)(2,1)}) fusion(bf16[1,2048,1024]{1,2,0:T(8,128)(2,1)S(1)} %copy-done.2, bf16[2048,1024]{0,1:T(8,128)(2,1)} %fusion.142, bf16[2,1024,3200]{2,1,0:T(8,128)(2,1)} %param.17, bf16[1,2048,3200]{2,1,0:T(8,128)(2,1)} %get-tuple-element.782), kind=kOutput, calls=%fused_computation.214 | convolution fusion | flops 13432256512 | bytes 32251904 | tf_op jit(solution)/vmap(transpose(jvp()))/dot_general | solution.py:21
  484.4 36.4 %convert_multiply_fusion = (bf16[1,2048,3200]{2,1,0:T(8,128)(2,1)}, bf16[1,2048,3200]{2,1,0:T(8,128)(2,1)}) fusion(f32[2048,3200]{1,0:T(8,128)} %fusion.173, f32[2048,3200]{1,0:T(8,128)} %get-tuple-element.302, bf16[2,3200,1024]{2,1,0:T(8,128)(2,1)} %param.15, bf16[1,2048,1024]{1,2,0:T(8,128)(2,1)S(1)} %fusion.185), kind=kOutput, calls=%fused_computation.168 | convolution fusion | flops 13526630400 | bytes 89391104 | tf_op jit(solution)/vmap(transpose(jvp()))/dot_general | solution.py:9
  520.8 242.9 %while.15 = (bf16[1,2048,3200]{2,1,0:T(8,128)(2,1)}, bf16[1,2048,1024]{1,2,0:T(8,128)(2,1)}, f32[3200,32]{0,1:T(8,128)S(1)}, f32[3200,32]{0,1:T(8,128)}, u32[]{:...) while((bf16[1,2048,3200]{2,1,0:T(8,128)(2,1)}, ...), condition=%wide.windowed_dot_general_cond_rs.3.clone, body=%wide.windowed_dot_general_body_rs.3.clone.sunk | while | flops 1679384576 | bytes 49349200 | solution.py:21
  526.5 7.2 fusion.309
  558.2 7.2 fusion.309
  588.5 7.2 fusion.309
  618.8 7.2 fusion.309
  649.1 7.2 fusion.309
  679.3 7.2 fusion.309
  709.6 7.2 fusion.309
  739.9 7.2 fusion.309
  763.7 254.7 %while.12 = (bf16[1,2048,3200]{2,1,0:T(8,128)(2,1)}, bf16[1,2048,1024]{1,2,0:T(8,128)(2,1)}, f32[3200,32]{0,1:T(8,128)S(1)}, f32[3200,32]{0,1:T(8,128)}, u32[]{:...) while((bf16[1,2048,3200]{2,1,0:T(8,128)(2,1)}, ...), condition=%wide.windowed_dot_general_cond_rs.clone, body=%wide.windowed_dot_general_body_rs.clone.sunk | while | flops 1679384576 | bytes 49349200 | solution.py:20
  769.2 7.2 fusion.285
  819.1 7.2 fusion.287
  850.8 7.2 fusion.287
  868.5 7.2 fusion.285
  882.1 7.2 fusion.287
  899.7 7.2 fusion.285
  913.4 7.2 fusion.287
  931.0 7.2 fusion.285
  944.7 7.2 fusion.287
  962.3 7.2 fusion.285
  976.0 7.2 fusion.287
  993.6 7.2 fusion.285
  1007.2 7.2 fusion.287
  1023.8 277.0 %while.13 = (bf16[1,2048,3200]{2,1,0:T(8,128)(2,1)}, bf16[1,2048,1024]{1,2,0:T(8,128)(2,1)}, f32[3200,32]{0,1:T(8,128)S(1)}, f32[3200,32]{0,1:T(8,128)}, u32[]{:...) while((bf16[1,2048,3200]{2,1,0:T(8,128)(2,1)}, ...), condition=%wide.windowed_dot_general_cond_rs.1.clone, body=%wide.windowed_dot_general_body_rs.1.clone.sunk | while | flops 1679384576 | bytes 49349200 | solution.py:20
  1029.6 7.2 fusion.293
  1051.5 8.5 collective-permute-done.6
  1074.5 8.4 collective-permute-done.4
  1107.6 7.2 fusion.293
  1114.9 10.8 collective-permute-done.4
  1138.4 11.0 collective-permute-done.6
  1156.8 7.2 fusion.293
  1169.5 7.2 fusion.295
  1184.7 7.2 fusion.293
  1216.4 7.2 fusion.293
  1230.1 7.2 fusion.295
  1277.0 7.2 fusion.293
  1300.8 18.3 copy.21
  1325.0 286.2 %while.16 = (bf16[1,2048,3200]{1,2,0:T(8,128)(2,1)}, bf16[1,2048,1024]{2,1,0:T(8,128)(2,1)}, f32[100,1024]{1,0:T(8,128)S(1)}, f32[100,1024]{1,0:T(8,128)S(1)}, u...) while((bf16[1,2048,3200]{1,2,0:T(8,128)(2,1)}, ...), condition=%wide.windowed_dot_general_cond_rs.4.clone, body=%wide.windowed_dot_general_body_rs.4.clone.sunk | while | flops 1681612800 | bytes 49349200 | solution.py:9
  1351.8 10.8 collective-permute-done.18
  1371.8 15.1 collective-permute-done.16
  1417.0 15.6 collective-permute-done.16
  1441.7 14.9 collective-permute-done.18
  1617.7 18.2 copy.23
  1635.9 246.6 %while.17 = (bf16[1,2048,1024]{2,1,0:T(8,128)(2,1)}, bf16[1,2048,3200]{1,2,0:T(8,128)(2,1)}, f32[1024,100]{0,1:T(8,128)S(1)}, f32[1024,100]{0,1:T(8,128)S(1)}, u...) while((bf16[1,2048,1024]{2,1,0:T(8,128)(2,1)}, ...), condition=%wide.windowed_dot_general_cond_rs.5.clone, body=%wide.windowed_dot_general_body_rs.5.clone.sunk | while | flops 1681612800 | bytes 49349200 | solution.py:9
  1883.9 10.1 collective-permute-done.29
  1900.8 91.0 %all-gather.14.cloned.1.call-done = bf16[1,2,3200,1024]{3,1,0,2:T(2,128)(2,1)} async-done(((bf16[1,2,100,1024]{3,1,0,2:T(2,128)(2,1)}), bf16[1,2,3200,1024]{3,1,0,2:T(2,128)(2,1)}) %all-gather.14.cloned.1.call-update) | async-done | bytes 13107216 | tf_op jit(solution)/reshape | solution.py:52
  1991.7 14.7 copy.44
  (721 shorter events, 1255.1 us)
Async XLA Ops:
  7.2 1893.6 %all-gather.12.cloned.1.call-start = ((), (), s32[]{:S(2)}) async-start(), calls=%async_computation.1 | async-start | bytes 13516800 | tf_op jit(solution)/reshape | solution.py:52
  430.8 587.6 %collective-permute-start.26 = (f32[3200,32]{0,1:T(8,128)}, f32[3200,32]{0,1:T(8,128)}, u32[]{:S(2)}, u32[]{:S(2)}) collective-permute-start(f32[3200,32]{0,1:T(8,128)} %get-tuple-element.41), channel_id=19, source_target_pairs={{0,1},{1,2},{2,3},{3,4},{4,5},{5,6},{6,7},{7,8},{8,9},{9,10},{10,1... | collective-permute-start | bytes 1228808 | tf_op jit(solution)/vmap(transpose(jvp()))/dot_general | solution.py:21
  763.7 255.7 %collective-permute-start.27 = (f32[3200,32]{0,1:T(8,128)}, f32[3200,32]{0,1:T(8,128)}, u32[]{:S(2)}, u32[]{:S(2)}) collective-permute-start(f32[3200,32]{0,1:T(8,128)} %get-tuple-element.43), channel_id=25, source_target_pairs={{0,1},{1,2},{2,3},{3,4},{4,5},{5,6},{6,7},{7,8},{8,9},{9,10},{10,1... | collective-permute-start | bytes 1228808 | tf_op jit(solution)/vmap(transpose(jvp()))/dot_general | solution.py:21
  763.7 19.7 collective-permute-start
  763.8 19.6 collective-permute-start.1
  1018.3 300.7 %collective-permute-start.24 = (f32[3200,32]{0,1:T(8,128)}, f32[3200,32]{0,1:T(8,128)}, u32[]{:S(2)}, u32[]{:S(2)}) collective-permute-start(f32[3200,32]{0,1:T(8,128)} %get-tuple-element.37), channel_id=6, source_target_pairs={{0,1},{1,2},{2,3},{3,4},{4,5},{5,6},{6,7},{7,8},{8,9},{9,10},{10,1... | collective-permute-start | bytes 1228808 | tf_op jit(solution)/vmap(transpose(jvp()))/dot_general | solution.py:20
  1023.7 877.0 %all-gather.10.cloned.1.call-start = ((), (), s32[]{:S(2)}) async-start(), calls=%async_computation | async-start | bytes 13516800 | tf_op jit(solution)/reshape | solution.py:52
  1038.8 21.1 %collective-permute-start.6 = (f32[3200,32]{0,1:T(8,128)S(1)}, f32[3200,32]{0,1:T(8,128)S(1)}, u32[]{:S(2)}, u32[]{:S(2)}) collective-permute-start(f32[3200,32]{0,1:T(8,128)S(1)} %get-tuple-element.503), channel_id=11, source_target_pairs={{0,1},{1,2},{2,3},{3,4},{4,5},{5,6},{6,7},{7,8},{8,9},{9,10},{10,1... | collective-permute-start | bytes 1228808 | tf_op jit(solution)/vmap(transpose(jvp()))/dot_general | solution.py:20
  1038.9 21.0 %collective-permute-start.7 = (f32[3200,32]{0,1:T(8,128)S(1)}, f32[3200,32]{0,1:T(8,128)S(1)}, u32[]{:S(2)}, u32[]{:S(2)}) collective-permute-start(f32[3200,32]{0,1:T(8,128)S(1)} %get-tuple-element.504), channel_id=10, source_target_pairs={{0,31},{1,0},{2,1},{3,2},{4,3},{5,4},{6,5},{7,6},{8,7},{9,8},{10,9... | collective-permute-start | bytes 1228808 | tf_op jit(solution)/vmap(transpose(jvp()))/dot_general | solution.py:20
  1061.8 21.1 %collective-permute-start.4 = (f32[3200,32]{0,1:T(8,128)S(1)}, f32[3200,32]{0,1:T(8,128)S(1)}, u32[]{:S(2)}, u32[]{:S(2)}) collective-permute-start(f32[3200,32]{0,1:T(8,128)S(1)} %broadcast_select_fusion.26), channel_id=9, source_target_pairs={{0,1},{1,2},{2,3},{3,4},{4,5},{5,6},{6,7},{7,8},{8,9},{9,10},{10,1... | collective-permute-start | bytes 1228808 | tf_op jit(solution)/vmap(transpose(jvp()))/dot_general | solution.py:20
  1061.9 23.4 %collective-permute-start.5 = (f32[3200,32]{0,1:T(8,128)S(1)}, f32[3200,32]{0,1:T(8,128)S(1)}, u32[]{:S(2)}, u32[]{:S(2)}) collective-permute-start(f32[3200,32]{0,1:T(8,128)S(1)} %broadcast_select_fusion.27), channel_id=8, source_target_pairs={{0,31},{1,0},{2,1},{3,2},{4,3},{5,4},{6,5},{7,6},{8,7},{9,8},{10,9... | collective-permute-start | bytes 1228808 | tf_op jit(solution)/vmap(transpose(jvp()))/dot_general | solution.py:20
  1102.2 23.6 %collective-permute-start.4 = (f32[3200,32]{0,1:T(8,128)S(1)}, f32[3200,32]{0,1:T(8,128)S(1)}, u32[]{:S(2)}, u32[]{:S(2)}) collective-permute-start(f32[3200,32]{0,1:T(8,128)S(1)} %broadcast_select_fusion.26), channel_id=9, source_target_pairs={{0,1},{1,2},{2,3},{3,4},{4,5},{5,6},{6,7},{7,8},{8,9},{9,10},{10,1... | collective-permute-start | bytes 1228808 | tf_op jit(solution)/vmap(transpose(jvp()))/dot_general | solution.py:20
  1102.3 23.4 %collective-permute-start.5 = (f32[3200,32]{0,1:T(8,128)S(1)}, f32[3200,32]{0,1:T(8,128)S(1)}, u32[]{:S(2)}, u32[]{:S(2)}) collective-permute-start(f32[3200,32]{0,1:T(8,128)S(1)} %broadcast_select_fusion.27), channel_id=8, source_target_pairs={{0,31},{1,0},{2,1},{3,2},{4,3},{5,4},{6,5},{7,6},{8,7},{9,8},{10,9... | collective-permute-start | bytes 1228808 | tf_op jit(solution)/vmap(transpose(jvp()))/dot_general | solution.py:20
  1125.8 23.6 %collective-permute-start.6 = (f32[3200,32]{0,1:T(8,128)S(1)}, f32[3200,32]{0,1:T(8,128)S(1)}, u32[]{:S(2)}, u32[]{:S(2)}) collective-permute-start(f32[3200,32]{0,1:T(8,128)S(1)} %get-tuple-element.503), channel_id=11, source_target_pairs={{0,1},{1,2},{2,3},{3,4},{4,5},{5,6},{6,7},{7,8},{8,9},{9,10},{10,1... | collective-permute-start | bytes 1228808 | tf_op jit(solution)/vmap(transpose(jvp()))/dot_general | solution.py:20
  1125.9 23.6 %collective-permute-start.7 = (f32[3200,32]{0,1:T(8,128)S(1)}, f32[3200,32]{0,1:T(8,128)S(1)}, u32[]{:S(2)}, u32[]{:S(2)}) collective-permute-start(f32[3200,32]{0,1:T(8,128)S(1)} %get-tuple-element.504), channel_id=10, source_target_pairs={{0,31},{1,0},{2,1},{3,2},{4,3},{5,4},{6,5},{7,6},{8,7},{9,8},{10,9... | collective-permute-start | bytes 1228808 | tf_op jit(solution)/vmap(transpose(jvp()))/dot_general | solution.py:20
  1193.7 15.4 collective-permute-start.6
  1193.7 15.3 collective-permute-start.7
  1300.7 19.4 collective-permute-start.25
  1324.9 666.8 %all-gather.14.cloned.1.call-start = ((), (), s32[]{:S(2)}) async-start(), calls=%async_computation.2 | async-start | bytes 13516800 | tf_op jit(solution)/reshape | solution.py:52
  1325.2 17.4 collective-permute-start.17
  1342.7 20.0 collective-permute-start.18
  1342.7 19.9 collective-permute-start.19
  1362.8 24.1 %collective-permute-start.16 = (f32[100,1024]{1,0:T(8,128)S(1)}, f32[100,1024]{1,0:T(8,128)S(1)}, u32[]{:S(2)}, u32[]{:S(2)}) collective-permute-start(f32[100,1024]{1,0:T(8,128)S(1)} %broadcast_select_fusion.32), channel_id=29, source_target_pairs={{0,1},{1,2},{2,3},{3,4},{4,5},{5,6},{6,7},{7,8},{8,9},{9,10},{10,1... | collective-permute-start | bytes 1228808 | tf_op jit(solution)/vmap(transpose(jvp()))/dot_general | solution.py:9
  1362.9 24.1 %collective-permute-start.17 = (f32[100,1024]{1,0:T(8,128)S(1)}, f32[100,1024]{1,0:T(8,128)S(1)}, u32[]{:S(2)}, u32[]{:S(2)}) collective-permute-start(f32[100,1024]{1,0:T(8,128)S(1)} %broadcast_select_fusion.33), channel_id=28, source_target_pairs={{0,31},{1,0},{2,1},{3,2},{4,3},{5,4},{6,5},{7,6},{8,7},{9,8},{10,9... | collective-permute-start | bytes 1228808 | tf_op jit(solution)/vmap(transpose(jvp()))/dot_general | solution.py:9
  1387.1 15.4 collective-permute-start.18
  1387.2 20.4 %collective-permute-start.19 = (f32[100,1024]{1,0:T(8,128)S(1)}, f32[100,1024]{1,0:T(8,128)S(1)}, u32[]{:S(2)}, u32[]{:S(2)}) collective-permute-start(f32[100,1024]{1,0:T(8,128)S(1)} %get-tuple-element.531), channel_id=30, source_target_pairs={{0,31},{1,0},{2,1},{3,2},{4,3},{5,4},{6,5},{7,6},{8,7},{9,8},{10,9... | collective-permute-start | bytes 1228808 | tf_op jit(solution)/vmap(transpose(jvp()))/dot_general | solution.py:9
  1407.8 24.8 %collective-permute-start.16 = (f32[100,1024]{1,0:T(8,128)S(1)}, f32[100,1024]{1,0:T(8,128)S(1)}, u32[]{:S(2)}, u32[]{:S(2)}) collective-permute-start(f32[100,1024]{1,0:T(8,128)S(1)} %broadcast_select_fusion.32), channel_id=29, source_target_pairs={{0,1},{1,2},{2,3},{3,4},{4,5},{5,6},{6,7},{7,8},{8,9},{9,10},{10,1... | collective-permute-start | bytes 1228808 | tf_op jit(solution)/vmap(transpose(jvp()))/dot_general | solution.py:9
  1407.9 24.7 %collective-permute-start.17 = (f32[100,1024]{1,0:T(8,128)S(1)}, f32[100,1024]{1,0:T(8,128)S(1)}, u32[]{:S(2)}, u32[]{:S(2)}) collective-permute-start(f32[100,1024]{1,0:T(8,128)S(1)} %broadcast_select_fusion.33), channel_id=28, source_target_pairs={{0,31},{1,0},{2,1},{3,2},{4,3},{5,4},{6,5},{7,6},{8,7},{9,8},{10,9... | collective-permute-start | bytes 1228808 | tf_op jit(solution)/vmap(transpose(jvp()))/dot_general | solution.py:9
  1432.7 23.8 %collective-permute-start.18 = (f32[100,1024]{1,0:T(8,128)S(1)}, f32[100,1024]{1,0:T(8,128)S(1)}, u32[]{:S(2)}, u32[]{:S(2)}) collective-permute-start(f32[100,1024]{1,0:T(8,128)S(1)} %get-tuple-element.530), channel_id=31, source_target_pairs={{0,1},{1,2},{2,3},{3,4},{4,5},{5,6},{6,7},{7,8},{8,9},{9,10},{10,1... | collective-permute-start | bytes 1228808 | tf_op jit(solution)/vmap(transpose(jvp()))/dot_general | solution.py:9
  1432.8 23.8 %collective-permute-start.19 = (f32[100,1024]{1,0:T(8,128)S(1)}, f32[100,1024]{1,0:T(8,128)S(1)}, u32[]{:S(2)}, u32[]{:S(2)}) collective-permute-start(f32[100,1024]{1,0:T(8,128)S(1)} %get-tuple-element.531), channel_id=30, source_target_pairs={{0,31},{1,0},{2,1},{3,2},{4,3},{5,4},{6,5},{7,6},{8,7},{9,8},{10,9... | collective-permute-start | bytes 1228808 | tf_op jit(solution)/vmap(transpose(jvp()))/dot_general | solution.py:9
  1471.7 15.7 collective-permute-start.18
  1471.8 15.7 collective-permute-start.19
  1502.7 15.6 collective-permute-start.18
  1502.8 15.5 collective-permute-start.19
  1533.8 15.5 collective-permute-start.18
  1533.8 15.4 collective-permute-start.19
  1549.5 15.2 collective-permute-start.16
  1564.8 15.4 collective-permute-start.18
  1564.8 15.3 collective-permute-start.19
  1580.4 15.3 collective-permute-start.16
  1580.5 15.2 collective-permute-start.17
  1595.8 15.3 collective-permute-start.18
  1595.9 15.2 collective-permute-start.19
  1611.2 271.7 %collective-permute-start.28 = (f32[100,1024]{1,0:T(8,128)S(1)}, f32[100,1024]{1,0:T(8,128)}, u32[]{:S(2)}, u32[]{:S(2)}) collective-permute-start(f32[100,1024]{1,0:T(8,128)S(1)} %get-tuple-element.45), channel_id=32, source_target_pairs={{0,1},{1,2},{2,3},{3,4},{4,5},{5,6},{6,7},{7,8},{8,9},{9,10},{10,1... | collective-permute-start | bytes 1228808 | tf_op jit(solution)/vmap(transpose(jvp()))/dot_general | solution.py:9
  1650.6 15.4 collective-permute-start.22
  1650.6 15.4 collective-permute-start.23
  1666.2 15.2 collective-permute-start.20
  1666.3 15.1 collective-permute-start.21
  1681.6 15.3 collective-permute-start.22
  1681.7 15.3 collective-permute-start.23
  1697.1 15.3 collective-permute-start.20
  1697.2 15.2 collective-permute-start.21
  1712.6 15.2 collective-permute-start.22
  1712.7 15.2 collective-permute-start.23
  1728.0 15.5 collective-permute-start.20
  1728.1 15.3 collective-permute-start.21
  1758.9 15.6 collective-permute-start.20
  1759.1 15.5 collective-permute-start.21
  1789.9 15.7 collective-permute-start.20
  1790.0 15.6 collective-permute-start.21
  1820.8 15.7 collective-permute-start.20
  1820.9 15.6 collective-permute-start.21
  1851.7 15.7 collective-permute-start.20
  1851.8 15.6 collective-permute-start.21
  (155 other events, 2475.4 us)
Sparse Core Ops, SparseCore 0:
  1023.9 129.0 all-gather.11
  1325.1 127.2 all-gather.9
  1897.8 93.8 all-gather.13
where the time goes:
time: 2040 us; the launch traced here: 2020 us
  matrix products  819 us (40%)
  starting transfers between devices  527 us (26%)
  waiting for transfers between devices  471 us (23%)
  other arithmetic  102 us (5%)
  local copies, waits for them, and re-layouts  87.4 us (4%)
    dot_general x35, matrix products, layer(): up = jnp.dot(a, w['w_up'], preferred_element_type=jnp.float32)  313 us
    dot_general x35, matrix products, layer(): gate = jnp.dot(a, w['w_gate'], preferred_element_type=jnp.float32)  295 us
    dot_general x66, waiting for transfers between devices, matmul(): jnp.dot(a, w, preferred_element_type=jnp.float32).astype(jnp.bfloat16)  250 us
    dot_general x35, matrix products, matmul(): jnp.dot(a, w, preferred_element_type=jnp.float32).astype(jnp.bfloat16)  211 us
    dot_general x66, starting transfers between devices, layer(): up = jnp.dot(a, w['w_up'], preferred_element_type=jnp.float32)  177 us
    dot_general x66, starting transfers between devices, layer(): gate = jnp.dot(a, w['w_gate'], preferred_element_type=jnp.float32)  176 us
    dot_general x66, starting transfers between devices, matmul(): jnp.dot(a, w, preferred_element_type=jnp.float32).astype(jnp.bfloat16)  174 us
    reshape x3, waiting for transfers between devices, step(): t.reshape(-1, *t.shape[2:])  91 us
  transfers between devices with their start and end apart: 201, of which 105 were waited for; matrix products, arithmetic and copies ran while one was open for 39% of the time, Pallas kernels for 0%

commit v1 on v0

v1 whole, which is shorter than its diff:
```python
import functools

import jax
import jax.numpy as jnp
from jax import lax
from jax.experimental import pallas as pl
from jax.experimental.pallas import tpu as pltpu
from jax.sharding import PartitionSpec as P

F32 = jnp.float32
BF16 = jnp.bfloat16
MESH = pl.DeviceIdType.MESH
WEIGHT = (16, 8, 4, 2, 1)
X, Y, Z1, Z0, CORE = range(5)
ORDERS = ((X, Y, Z0, Z1), (Y, X, Z0, Z1), (Z0, Z1, X, Y))
COLUMNS = ((0, 1280), (1280, 1280), (2560, 640))
ROWS = ((0, 80), (80, 80), (160, 40))
ROWWISE, COLWISE = (32, 3200), (200, 512)
KINDS = ("d", "g", "u")


def dot(a, b, ca, cb):
    return lax.dot_general(a, b, (((ca,), (cb,)), ((), ())), preferred_element_type=F32)


def norm(h):
    wide = h.astype(F32)
    scale = lax.rsqrt(jnp.mean(wide**2, -1, keepdims=True) + 1e-6)
    return (wide * scale).astype(BF16), scale


def adamw(w, m, v, g):
    m = 0.9 * m + 0.1 * g
    v = 0.95 * v + 0.05 * g * g
    step = m * lax.rsqrt(v + 1e-8) + 0.1 * w
    return (w - 0.02 * step).astype(BF16), m, v


def half_of(kind):
    return COLWISE if kind == "d" else ROWWISE


def part_of(kind, color):
    rows, columns = half_of(kind)
    if kind == "d":
        at, n = ROWS[color]
        return (pl.ds(at, n), slice(None)), (n, columns)
    at, n = COLUMNS[color]
    return (slice(None), pl.ds(at, n)), (rows, n)


def place():
    me = lax.axis_index("dp")
    bits = tuple(lax.rem(lax.div(me, w), 2) for w in WEIGHT)
    partners = tuple(me + (1 - 2 * b) * w for b, w in zip(bits, WEIGHT))
    return bits, partners


def greet(partners):
    barrier = pltpu.get_barrier_semaphore()
    for p in partners:
        pl.semaphore_signal(barrier, inc=1, device_id={"dp": p}, device_id_type=MESH)
    pl.semaphore_wait(barrier, len(partners))


def remote(src, dst, send, recv, to):
    return pltpu.make_async_remote_copy(src_ref=src, dst_ref=dst, send_sem=send, recv_sem=recv, device_id={"dp": to}, device_id_type=MESH)


def free_of(index):
    return [i for i in range(4) if index[i] is None]


def for_blocks(index, body):
    free = free_of(index)

    def one(n, _):
        at = list(index)
        for k, i in enumerate(free):
            at[i] = lax.rem(lax.div(n, 2 ** (len(free) - 1 - k)), 2)
        body(tuple(at))
        return 0

    lax.fori_loop(0, 2 ** len(free), one, 0)


def window(index):
    return tuple(slice(None) if i is None else i for i in index)


def reduce_kernel(kinds, *refs):
    n = len(kinds)
    grads, outs, refs = refs[:n], refs[n : 2 * n], refs[2 * n :]
    totals, firsts, refs = refs[:n], refs[n : 2 * n], refs[2 * n :]
    gots, refs = [refs[12 * u : 12 * u + 12] for u in range(n)], refs[12 * n :]
    last, send, recv, local = refs
    bits, partners = place()
    core = bits[CORE]
    greet(partners)

    def halves(u, which):
        if kinds[u] == "d":
            return grads[u].at[:, :, :, :, :, pl.ds(pl.multiple_of(which * 512, 512), 512)]
        return grads[u].at[:, :, :, :, which]

    started = {}
    for u in range(n):
        copy = remote(halves(u, 1 - core), firsts[u], send.at[u, 12], recv.at[u, 12], partners[CORE])
        copy.start()
        own = pltpu.make_async_copy(halves(u, core), totals[u], local.at[u])
        own.start()
        started[u] = (copy, own)

    state = {(u, color): [None] * 4 for u in range(n) for color in range(3)}
    flying = {}

    def total(u, color, at, steps):
        where = (*at, *part_of(kinds[u], color)[0])
        value = totals[u][where].astype(F32) + firsts[u][where].astype(F32)
        for s in range(steps):
            rest = tuple(at[i] for i in range(4) if i not in ORDERS[color][: s + 1])
            got = gots[u][color * 4 + s]
            value += (got[rest] if rest else got[...]).astype(F32)
        return value.astype(BF16)

    def launch(u, color, s):
        dim = ORDERS[color][s]
        part, _ = part_of(kinds[u], color)
        index = list(state[u, color])
        index[dim] = 1 - bits[dim]
        k = color * 4 + s

        def ready(at):
            totals[u][(*at, *part)] = total(u, color, at, s)

        for_blocks(index, ready)
        copy = remote(totals[u].at[(*window(index), *part)], gots[u][k], send.at[u, k], recv.at[u, k], partners[dim])
        copy.start()
        flying[u, color] = copy
        index[dim] = bits[dim]
        state[u, color] = index

    waits = []
    for t in range(n + 4):
        for u in reversed(range(n)):
            s = t - u
            if s == 0:
                copy, own = started[u]
                own.wait()
                copy.wait_recv()
                waits.append(copy)
                for color in range(3):
                    launch(u, color, 0)
            elif 0 < s <= 4:
                for color in range(3):
                    copy = flying[u, color]
                    copy.wait_recv()
                    waits.append(copy)
                    if s < 4:
                        launch(u, color, s)
                        continue
                    (rows, columns), _ = part_of(kinds[u], color)
                    if kinds[u] == "d":
                        last[rows, pl.ds(pl.multiple_of(core * 512, 512), 512)] = total(u, color, bits[:4], 4)
                    else:
                        outs[u][rows, columns] = total(u, color, bits[:4], 4)
                if s == 4:
                    if kinds[u] == "d":
                        columns = (slice(None), pl.ds(pl.multiple_of(core * 512, 512), 512))
                        copy = remote(last.at[columns], last.at[columns], send.at[u, 13], recv.at[u, 13], partners[CORE])
                        copy.start()
                        flying["d"] = copy
    for u in range(n):
        if kinds[u] == "d":
            copy = flying["d"]
            copy.wait_recv()
            waits.append(copy)
            outs[u][...] = last[...]
    for copy in waits:
        copy.wait_send()


def reduce_scatter(grads, kinds, collective_id):
    n = len(kinds)
    blocks = lambda shape: pltpu.VMEM((2, 2, 2, 2, *shape), BF16)
    scratch = [blocks(half_of(k)) for k in kinds] * 2
    for k in kinds:
        for color in range(3):
            for s in range(4):
                scratch.append(pltpu.VMEM((2,) * (3 - s) + part_of(k, color)[1], BF16))
    scratch += [pltpu.VMEM((200, 1024), BF16), pltpu.SemaphoreType.DMA((n, 14)), pltpu.SemaphoreType.DMA((n, 14)), pltpu.SemaphoreType.DMA((n,))]
    return pl.pallas_call(
        functools.partial(reduce_kernel, kinds),
        out_shape=[jax.ShapeDtypeStruct((200, 1024) if k == "d" else (32, 3200), BF16) for k in kinds],
        in_specs=[pl.BlockSpec(memory_space=pltpu.HBM)] * n,
        out_specs=[pl.BlockSpec(memory_space=pltpu.VMEM)] * n,
        scratch_shapes=scratch,
        compiler_params=pltpu.CompilerParams(collective_id=collective_id, has_side_effects=True, vmem_limit_bytes=60 * 2**20),
        name=f"reduce_{collective_id}",
    )(*grads)


def gather_kernel(units, *refs):
    n = len(units)
    blocks, outs, (send, recv, local) = refs[:n], refs[n : n + 3], refs[n + 3 :]
    bits, partners = place()
    core = bits[CORE]
    greet(partners)

    def at(u, index, color):
        kind, layer = units[u]
        (rows, columns), _ = part_of(kind, color)
        out = outs[KINDS.index(kind)]
        if kind == "d":
            return out.at[(layer, *window(index), rows, pl.ds(pl.multiple_of(core * 512, 512), 512))]
        return out.at[(layer, *window(index), core, rows, columns)]

    sent = []
    flying = {}
    state = {}

    def across(u, color, src, index, k):
        dst = at(u, index, color)
        copy = remote(dst if src is None else src, dst, send.at[u, 9 * color + k], recv.at[u, 9 * color + k], partners[CORE])
        copy.start()
        sent.append((copy, True))

    def launch(u, color, s, src=None):
        dim = ORDERS[color][3 - s]
        dst = at(u, state[u, color], color)
        copy = remote(dst if src is None else src, dst, send.at[u, 9 * color + s], recv.at[u, 9 * color + s], partners[dim])
        copy.start()
        flying[u, color] = copy

    for t in range(n + 4):
        for u in reversed(range(n)):
            s = t - u
            if s == 0:
                kind, layer = units[u]
                for color in range(3):
                    state[u, color] = list(bits[:4])
                    (rows, columns), _ = part_of(kind, color)
                    src = blocks[u].at[rows, columns]
                    launch(u, color, 0, src)
                    across(u, color, src, state[u, color], 4)
                    own = pltpu.make_async_copy(src, at(u, state[u, color], color), local.at[u, color])
                    own.start()
                    flying["own", u, color] = own
            elif 0 < s <= 4:
                for color in range(3):
                    copy = flying[u, color]
                    copy.wait_recv()
                    sent.append((copy, False))
                    if s == 1:
                        flying["own", u, color].wait()
                    dim = ORDERS[color][4 - s]
                    fresh = list(state[u, color])
                    fresh[dim] = 1 - bits[dim]
                    state[u, color][dim] = None
                    if s < 4:
                        launch(u, color, s)
                    across(u, color, None, fresh, 4 + s)
    for copy, from_core in sent:
        copy.wait_send()
        if from_core:
            copy.wait_recv()


def all_gather(blocks, units, layers, collective_id):
    n = len(units)
    shapes = [(layers, 2, 2, 2, 2, 200, 1024)] + [(layers, 2, 2, 2, 2, 2, 32, 3200)] * 2
    return pl.pallas_call(
        functools.partial(gather_kernel, units),
        out_shape=[jax.ShapeDtypeStruct(s, BF16) for s in shapes],
        in_specs=[pl.BlockSpec(memory_space=pltpu.VMEM)] * n,
        out_specs=[pl.BlockSpec(memory_space=pltpu.HBM)] * 3,
        scratch_shapes=[pltpu.SemaphoreType.DMA((n, 27)), pltpu.SemaphoreType.DMA((n, 27)), pltpu.SemaphoreType.DMA((n, 3))],
        compiler_params=pltpu.CompilerParams(collective_id=collective_id, has_side_effects=True),
        name=f"gather_{collective_id}",
    )(*blocks)


def solution(mesh):
    def local(x, dy, wg, wu, wd, mg, mu, md, vg, vu, vd):
        x, dy = x[0], dy[0]
        me = lax.axis_index("dp")
        core = lax.rem(me, 2)
        layers = wg.shape[0]
        old = {"g": (wg, mg, vg), "u": (wu, mu, vu), "d": (wd, md, vd)}

        h = x
        saved = []
        for i in range(layers):
            a, scale = norm(h)
            gate = dot(a, wg[i], 1, 0)
            up = dot(a, wu[i], 1, 0)
            act = (jax.nn.silu(gate) * up).astype(BF16)
            saved.append((h, a, scale, gate, up, act))
            if i + 1 < layers:
                h = h + dot(act, wd[i], 1, 0).astype(BF16)
        d = dy
        summed = {}
        for i in reversed(range(layers)):
            h, a, scale, gate, up, act = saved[i]
            by_d = dot(act, d, 0, 0).astype(BF16)
            d_act = dot(d, wd[i], 1, 1).astype(BF16).astype(F32)
            sig = jax.nn.sigmoid(gate)
            d_up = (d_act * (gate * sig)).astype(BF16)
            d_gate = (d_act * up * (sig * (1 + gate * (1 - sig)))).astype(BF16)
            by_g = dot(a, d_gate, 0, 0).astype(BF16)
            by_u = dot(a, d_up, 0, 0).astype(BF16)
            grads = [by_d.reshape(2, 2, 2, 2, 200, 1024)] + [t.reshape(2, 2, 2, 2, 2, 32, 3200) for t in (by_g, by_u)]
            summed[i] = dict(zip(KINDS, reduce_scatter(grads, KINDS, i)))
            if i:
                da = dot(d_gate, wg[i], 1, 1).astype(BF16) + dot(d_up, wu[i], 1, 1).astype(BF16)
                da = da.astype(F32)
                wide = h.astype(F32)
                inner = jnp.mean(da * wide, -1, keepdims=True)
                d = d + (scale * da - wide * (scale**3 * inner)).astype(BF16)
        new = {}
        for kind in KINDS:
            w, m, v = old[kind]
            rows = m.shape[1]
            g = jnp.stack([summed[i][kind] for i in range(layers)])
            if kind == "d":
                g = lax.dynamic_slice_in_dim(g, core * rows, rows, 1)
            mine = lax.dynamic_slice_in_dim(w, me * rows, rows, 1)
            new[kind] = adamw(mine.astype(F32), m, v, g.astype(F32))
        mine = new["d"][0]
        other = lax.ppermute(mine, "dp", [(k, k + 1 - 2 * (k % 2)) for k in range(32)])
        first = core == 0
        whole = jnp.concatenate([jnp.where(first, mine, other), jnp.where(first, other, mine)], 1)
        part = {"d": lax.dynamic_slice_in_dim(whole, core * 512, 512, 2), "g": new["g"][0], "u": new["u"][0]}
        units = tuple((kind, i) for i in reversed(range(layers)) for kind in KINDS)
        full = all_gather([part[kind][i] for kind, i in units], units, layers, 2)
        full = {kind: t.reshape(old[kind][0].shape) for kind, t in zip(KINDS, full)}
        return tuple(full[k] for k in "gud") + tuple(new[k][1] for k in "gud") + tuple(new[k][2] for k in "gud")

    seq, whole, rows = P(("rep", "dp")), P(), P(None, "dp")
    return jax.shard_map(
        local,
        mesh=mesh,
        in_specs=(seq, seq, whole, whole, whole) + (rows,) * 6,
        out_specs=(P("rep"),) * 3 + (P("rep", "dp"),) * 6,
        check_vma=False,
    )
```

time: 2040 us -> 810 us (0.40)
  starting transfers between devices: 527 us -> 0.17 us
  waiting for transfers between devices: 471 us -> 0.01 us
  matrix products: 819 us -> 367 us
  Pallas kernels: 0 us -> 371 us
  other arithmetic: 102 us -> 15.8 us
  local copies, waits for them, and re-layouts: 87.4 us -> 47.2 us
    dot_general x198 -> x0, starting transfers between devices: 527 us -> none  [the longest x66 177 us: layer(): up = jnp.dot(a, w['w_up'], preferred_element_type=jnp.float32)]
    dot_general x105 -> x15, matrix products: 819 us -> 367 us  [dot(): lax.dot_general(a, b, (((ca,), (cb,)), ((), ())), preferred_element_type=...]
    dot_general x198 -> x0, waiting for transfers between devices: 380 us -> none  [the longest x66 250 us: matmul(): jnp.dot(a, w, preferred_element_type=jnp.float32).astype(jnp.bfloat16)]
    pallas_call x0 -> x3, Pallas kernels: none -> 371 us  [the longest x2 199 us: reduce_scatter(): pl.pallas_call(functools.partial(reduce_kernel, kinds), out_shape=[jax.Sh...]
    reshape x3 -> x0, waiting for transfers between devices: 91 us -> none  [step(): t.reshape(-1, *t.shape[2:])]
    dot_general x192 -> x0, other arithmetic: 72.8 us -> none
    unnamed x45 -> x41, local copies, waits for them, and re-layouts: 71.5 us -> 44.8 us
  transfers between devices with their start and end apart: 201 -> 1, of which waited for: 105 -> 0; matrix products, arithmetic and copies ran while one was open for 39% -> 1% of each run, Pallas kernels for 0% -> 0%
where the time goes in v1:
time: 810 us; the launch traced here: 803 us
  Pallas kernels  371 us (46%)
  matrix products  367 us (45%)
  local copies, waits for them, and re-layouts  47.2 us (6%)
  other arithmetic  15.8 us (2%)
    dot_general x15, matrix products, dot(): lax.dot_general(a, b, (((ca,), (cb,)), ((), ())), preferred_element_type=...  367 us
    pallas_call x2, Pallas kernels, reduce_scatter(): pl.pallas_call(functools.partial(reduce_kernel, kinds), out_shape=[jax.Sh...  199 us
    pallas_call x1, Pallas kernels, all_gather(): pl.pallas_call(functools.partial(gather_kernel, units), out_shape=[jax.Sh...  172 us
    unnamed x41, local copies, waits for them, and re-layouts  44.8 us
  transfers between devices with their start and end apart: 1, of which 0 were waited for; matrix products, arithmetic and copies ran while one was open for 1% of the time, Pallas kernels for 0%

profile of v1, /device:TPU:0, one launch (start us, length us, event | category | flops | bytes accessed | tf_op | source)
XLA Modules:
  0.0 803.1 jit_solution(9858551444179111269)
XLA Ops:
  0.6 6.5 copy.21
  7.2 3.1 fusion.13
  10.2 0.0 copy-start.11
  10.3 21.9 %fusion.41 = f32[2048,3200]{1,0:T(8,128)} fusion(bf16[2,1024,3200]{2,1,0:T(8,128)(2,1)} %param.13, bf16[1,2048,1024]{2,1,0:T(8,128)(2,1)} %param.11, f32[2048]{0:T(1024)S(1)} %add_rsqrt_fusion.1), kind=kOutput, calls=%fused_computation.56 | convolution fusion | flops 13428064256 | bytes 36970496 | tf_op jit(solution)/shard_map/dot_general | solution.py:23
  32.1 0.0 copy-done.11
  32.1 32.1 %multiply_convert_fusion.1 = (bf16[2048,3200]{1,0:T(8,128)(2,1)}, f32[2048,3200]{1,0:T(8,128)}) fusion(f32[2048,3200]{1,0:T(8,128)} %fusion.41, bf16[2,1024,3200]{2,1,0:T(8,128)(2,1)} %param.14, bf16[1,2048,1024]{2,1,0:T(8,128)(2,1)} %param.11, f32[2048]{0:T(1024)S(1)} %add_rsqrt_fusion.1), kind=kOutput, calls=%fused_computation.13 | convolution fusion | flops 13467385856 | bytes 76292096 | tf_op jit(solution)/shard_map/dot_general | solution.py:23
  64.2 22.0 %fusion.17 = (f32[2048]{0:T(1024)S(1)}, bf16[2048,1024]{0,1:T(8,128)(2,1)}) fusion(bf16[2048,3200]{1,0:T(8,128)(2,1)} %get-tuple-element.55, bf16[2,3200,1024]{2,1,0:T(8,128)(2,1)} %param.15, bf16[1,2048,1024]{1,2,0:T(8,128)(2,1)} %copy.21), kind=kOutput, calls=%fused_computation.32 | convolution fusion | flops 13432256512 | bytes 28057600 | tf_op jit(solution)/shard_map/dot_general | solution.py:23
  86.3 0.0 copy-start.8
  86.3 0.0 copy-start.3
  86.3 23.5 %fusion.33 = f32[2048,3200]{1,0:T(8,128)} fusion(bf16[2,1024,3200]{2,1,0:T(8,128)(2,1)} %param.14, bf16[2048,1024]{0,1:T(8,128)(2,1)} %get-tuple-element.58, f32[2048]{0:T(1024)S(1)} %add_rsqrt_fusion), kind=kOutput, calls=%fused_computation.48 | convolution fusion | flops 13428064256 | bytes 36970496 | tf_op jit(solution)/shard_map/dot_general | solution.py:23
  109.7 0.0 copy-done.8
  109.7 0.0 copy-done.3
  109.7 20.8 %fusion.29 = f32[2048,3200]{1,0:T(8,128)} fusion(bf16[2,1024,3200]{2,1,0:T(8,128)(2,1)} %param.13, bf16[2048,1024]{0,1:T(8,128)(2,1)S(1)} %copy-done.3, f32[2048]{0:T(1024)S(1)} %add_rsqrt_fusion), kind=kOutput, calls=%fused_computation.44 | convolution fusion | flops 13428064256 | bytes 36970496 | tf_op jit(solution)/shard_map/dot_general | solution.py:23
  130.5 26.0 %fusion.26 = bf16[3200,1024]{1,0:T(8,128)(2,1)} fusion(f32[2048,3200]{1,0:T(8,128)} %fusion.33, f32[2048,3200]{1,0:T(8,128)} %fusion.29, bf16[1,2048,1024]{2,1,0:T(8,128)(2,1)} %param.12), kind=kOutput, calls=%fused_computation.38 | convolution fusion | flops 13464371200 | bytes 63176704 | tf_op jit(solution)/shard_map/dot_general | solution.py:23
  156.5 0.0 copy-start.4
  156.5 39.0 %fusion.2 = (bf16[2048,3200]{1,0:T(8,128)(2,1)}, bf16[2048,3200]{1,0:T(8,128)(2,1)}) fusion(f32[2048,3200]{1,0:T(8,128)} %fusion.29, f32[2048,3200]{1,0:T(8,128)} %fusion.33, bf16[2,3200,1024]{2,1,0:T(8,128)(2,1)} %param.15, bf16[1,2048,1024]{2,1,0:T(8,128)(2,1)} %param.12), kind=kOutput, calls=%fused_computation.6 | convolution fusion | flops 13520076800 | bytes 89391104 | tf_op jit(solution)/shard_map/dot_general | solution.py:23
  195.4 0.0 copy-done.4
  195.4 0.0 copy-start.10
  195.4 20.6 %convolution_convert_fusion.3 = bf16[1024,3200]{1,0:T(8,128)(2,1)} fusion(bf16[2048,3200]{1,0:T(8,128)(2,1)} %get-tuple-element.46, bf16[2048,1024]{0,1:T(8,128)(2,1)S(1)} %copy-done.4, f32[2048]{0:T(1024)S(1)} %add_rsqrt_fusion), kind=kOutput, calls=%fused_computation.40 | convolution fusion | flops 13431341056 | bytes 23863296 | tf_op jit(solution)/shard_map/dot_general | solution.py:23
  216.0 0.0 copy-done.10
  216.0 17.8 %fusion.27 = bf16[2048,1024]{0,1:T(8,128)(2,1)} fusion(bf16[2048,3200]{1,0:T(8,128)(2,1)} %get-tuple-element.46, bf16[2,1024,3200]{2,1,0:T(8,128)(2,1)S(1)} %copy-done.10), kind=kOutput, calls=%fused_computation.42 | convolution fusion | flops 13421772800 | bytes 23855104 | tf_op jit(solution)/shard_map/dot_general | solution.py:23
  233.9 6.5 copy.22
  240.4 21.0 %convolution_convert_fusion.2 = bf16[1024,3200]{1,0:T(8,128)(2,1)} fusion(bf16[2048,3200]{1,0:T(8,128)(2,1)} %get-tuple-element.45, bf16[2048,1024]{0,1:T(8,128)(2,1)} %get-tuple-element.58, f32[2048]{0:T(1024)S(1)} %add_rsqrt_fusion), kind=kOutput, calls=%fused_computation.39 | convolution fusion | flops 13431341056 | bytes 23863296 | tf_op jit(solution)/shard_map/dot_general | solution.py:23
  261.4 23.1 %fusion.19 = (f32[2048]{0:T(1024)S(1)}, bf16[2048,1024]{0,1:T(8,128)(2,1)}) fusion(bf16[2048,1024]{0,1:T(8,128)(2,1)} %get-tuple-element.58, bf16[2048,1024]{0,1:T(8,128)(2,1)} %fusion.27, bf16[2048,3200]{1,0:T(8,128)(2,1)} %get-tuple-element.45, bf16[2,1024,3200]{2,1,0:T(8,128)(2,1)} %param.14), kind=kOutput, calls=%fused_computation.34 | convolution fusion | flops 13434353664 | bytes 32251904 | tf_op jit(solution)/shard_map/dot_general | solution.py:23
  284.5 0.0 copy-done.9
  284.5 0.0 copy-done
  284.5 5.3 fusion.55
  289.8 0.0 copy-start.5
  289.8 2.0 copy-done.5
  291.8 19.7 %convolution_convert_fusion.4 = bf16[3200,1024]{1,0:T(8,128)(2,1)} fusion(bf16[2048,3200]{1,0:T(8,128)(2,1)} %get-tuple-element.55, bf16[2048,1024]{0,1:T(8,128)(2,1)S(1)} %fusion.55), kind=kOutput, calls=%fused_computation.41 | convolution fusion | flops 13425049600 | bytes 23855104 | tf_op jit(solution)/shard_map/dot_general | solution.py:23
  311.5 21.0 %convolution_convert_fusion = bf16[2048,3200]{1,0:T(8,128)(2,1)} fusion(bf16[2048,1024]{0,1:T(8,128)(2,1)} %copy-done.5, bf16[2,3200,1024]{2,1,0:T(8,128)(2,1)} %param.15), kind=kOutput, calls=%fused_computation.16 | convolution fusion | flops 13428326400 | bytes 23855104 | tf_op jit(solution)/shard_map/dot_general | solution.py:23
  332.6 0.0 copy-done.12
  332.6 29.5 %fusion.23 = bf16[1024,3200]{1,0:T(8,128)(2,1)} fusion(bf16[2048,3200]{1,0:T(8,128)(2,1)} %convolution_convert_fusion, f32[2048,3200]{1,0:T(8,128)} %fusion.41, bf16[1,2048,1024]{1,2,0:T(8,128)(2,1)} %copy.21, f32[2048]{0:T(1024)S(1)} %copy-done.12), kind=kOutput, calls=%fused_computation.37 | convolution fusion | flops 13477216256 | bytes 50077696 | tf_op jit(solution)/shard_map/dot_general | solution.py:23
  362.0 0.0 copy-done.1
  362.0 29.4 %fusion.20 = bf16[1024,3200]{1,0:T(8,128)(2,1)} fusion(f32[2048,3200]{1,0:T(8,128)} %get-tuple-element.56, bf16[2048,3200]{1,0:T(8,128)(2,1)} %convolution_convert_fusion, f32[2048,3200]{1,0:T(8,128)} %fusion.41, bf16[1,2048,1024]{1,2,0:T(8,128)(2,1)S(1)} %copy-done.1, f32[2048]{0:T(1024)S(1)} %copy-done.12), kind=kOutput, calls=%fused_computation.36 | convolution fusion | flops 13503430656 | bytes 76292096 | tf_op jit(solution)/shard_map/dot_general | solution.py:23
  391.4 101.9 %reduce_1.1 = (bf16[200,1024]{1,0:T(8,128)(2,1)}, bf16[32,3200]{1,0:T(8,128)(2,1)}, bf16[32,3200]{1,0:T(8,128)(2,1)}) custom-call(bf16[2,2,2,2,200,1024]{5,4,3,2,1,0:T(8,128)(2,1)} %bitcast.98, bf16[2,2,2,2,2,32,3200]{6,5,4,3,2,1,0:T(8,128)(2,1)} %bitcast.99, bf16[2,2,2,2,2,32,3200]{6,5,4,3,2,1,0:T(8,128)(2,1)} %bitcast.100), custom_call_target="tpu_custom_call" | custom-call | tf_op jit(solution)/shard_map/reduce_1/pallas_call | solution.py:192
  493.3 0.0 copy-start.7
  493.3 0.0 copy-start.6
  493.3 97.5 %reduce_0.1 = (bf16[200,1024]{1,0:T(8,128)(2,1)}, bf16[32,3200]{1,0:T(8,128)(2,1)}, bf16[32,3200]{1,0:T(8,128)(2,1)}) custom-call(bf16[2,2,2,2,200,1024]{5,4,3,2,1,0:T(8,128)(2,1)} %bitcast.101, bf16[2,2,2,2,2,32,3200]{6,5,4,3,2,1,0:T(8,128)(2,1)} %bitcast.103, bf16[2,2,2,2,2,32,3200]{6,5,4,3,2,1,0:T(8,128)(2,1)} %bitcast.102), custom_call_target="tpu_custom_call" | custom-call | tf_op jit(solution)/shard_map/reduce_0/pallas_call | solution.py:192
  590.9 0.0 copy-done.7
  590.9 2.7 fusion.72
  593.6 0.2 collective-permute-start
  593.8 0.0 copy-done.6
  593.8 4.5 fusion.77
  598.2 0.8 slice_bitcast_fusion.1
  599.0 0.8 slice_bitcast_fusion
  599.8 1.5 copy.24
  601.3 1.5 copy.25
  602.9 0.0 collective-permute-done
  602.9 0.1 broadcast_select_fusion
  602.9 0.2 fusion.86
  603.1 0.8 slice_bitcast_fusion.2
  603.9 172.0 %gather_2.1 = (bf16[2,2,2,2,2,200,1024]{6,5,4,3,2,1,0:T(8,128)(2,1)}, bf16[2,2,2,2,2,2,32,3200]{7,6,5,4,3,2,1,0:T(8,128)(2,1)}, bf16[2,2,2,2,2,2,32,3200]{7,6,5,4,3,2,1,0:T(8,128)(2,1)}) custom-call(bf16[200,512]{1,0:T(8,128)(2,1)} %get-tuple-element.54.refs_0_, bf16[32,3200]{1,0:T(8,128)(2,1)} %get-tuple-element.52.refs_1_, ...), custom_call_target="tpu_custom_call" | custom-call | tf_op jit(solution)/shard_map/gather_2/pallas_call | solution.py:272
  775.9 0.0 copy-start.2
  775.9 0.0 slice-start
  775.9 0.0 slice-start.1
  775.9 12.7 %copy.37 = bf16[2,1024,3200]{2,1,0:T(8,128)(2,1)} copy(bf16[2,1024,3200]{2,1,0:T(8,128)(2,1)} %bitcast.97) | data formatting | bytes 26214400
  788.6 0.0 copy-done.2
  788.6 6.6 copy.38
  795.3 0.0 slice-done
  795.3 1.2 slice-done.1
  796.4 1.3 slice-done.2
  797.7 0.0 slice-done.3
  797.7 4.9 copy.39
  (10 shorter events, 0.0 us)
Async XLA Ops:
  10.2 21.9 %copy-start.11 = (f32[2048]{0:T(1024)}, f32[2048]{0:T(1024)S(1)}, u32[]{:S(2)}) copy-start(f32[2048]{0:T(1024)S(1)} %add_rsqrt_fusion.1) | copy-start | bytes 24580
  86.3 23.5 %copy-start.8 = (f32[2048]{0:T(1024)}, f32[2048]{0:T(1024)S(1)}, u32[]{:S(2)}) copy-start(f32[2048]{0:T(1024)S(1)} %get-tuple-element.57) | copy-start | bytes 24580
  86.3 23.5 %copy-start.3 = (bf16[2048,1024]{0,1:T(8,128)(2,1)S(1)}, bf16[2048,1024]{0,1:T(8,128)(2,1)}, u32[]{:S(2)}) copy-start(bf16[2048,1024]{0,1:T(8,128)(2,1)} %get-tuple-element.58) | copy-start | bytes 12582916
  156.5 39.0 %copy-start.4 = (bf16[2048,1024]{0,1:T(8,128)(2,1)S(1)}, bf16[2048,1024]{0,1:T(8,128)(2,1)}, u32[]{:S(2)}) copy-start(bf16[2048,1024]{0,1:T(8,128)(2,1)} %get-tuple-element.58) | copy-start | bytes 12582916
  195.4 20.6 %copy-start.10 = (bf16[2,1024,3200]{2,1,0:T(8,128)(2,1)S(1)}, bf16[2,1024,3200]{2,1,0:T(8,128)(2,1)}, u32[]{:S(2)}) copy-start(bf16[2,1024,3200]{2,1,0:T(8,128)(2,1)} %param.13) | copy-start | bytes 39321604
  261.4 23.1 %copy-start.9 = (f32[2048]{0:T(1024)S(1)}, f32[2048]{0:T(1024)}, u32[]{:S(2)}) copy-start(f32[2048]{0:T(1024)} %copy-done.8) | copy-start | bytes 24580
  261.4 23.1 %copy-start = (bf16[1,2048,1024]{1,2,0:T(8,128)(2,1)S(1)}, bf16[1,2048,1024]{1,2,0:T(8,128)(2,1)}, u32[]{:S(2)}) copy-start(bf16[1,2048,1024]{1,2,0:T(8,128)(2,1)} %copy.22) | copy-start | bytes 12582916
  289.8 2.0 copy-start.5
  311.5 21.0 %copy-start.12 = (f32[2048]{0:T(1024)S(1)}, f32[2048]{0:T(1024)}, u32[]{:S(2)}) copy-start(f32[2048]{0:T(1024)} %copy-done.11) | copy-start | bytes 24580
  332.6 29.5 %copy-start.1 = (bf16[1,2048,1024]{1,2,0:T(8,128)(2,1)S(1)}, bf16[1,2048,1024]{1,2,0:T(8,128)(2,1)}, u32[]{:S(2)}) copy-start(bf16[1,2048,1024]{1,2,0:T(8,128)(2,1)} %copy.21) | copy-start | bytes 12582916
  493.3 97.6 %copy-start.7 = (bf16[200,1024]{1,0:T(8,128)(2,1)S(1)}, bf16[200,1024]{1,0:T(8,128)(2,1)}, u32[]{:S(2)}) copy-start(bf16[200,1024]{1,0:T(8,128)(2,1)} %get-tuple-element.19) | copy-start | bytes 1228804
  493.3 100.4 %copy-start.6 = (f32[2,32,3200]{2,1,0:T(8,128)S(1)}, f32[2,32,3200]{2,1,0:T(8,128)}, u32[]{:S(2)}) copy-start(f32[2,32,3200]{2,1,0:T(8,128)} %param.19) | copy-start | bytes 2457604
  593.6 9.3 %collective-permute-start = (bf16[2,100,1024]{2,1,0:T(8,128)(2,1)S(1)}, bf16[2,100,1024]{2,1,0:T(8,128)(2,1)S(1)}, u32[]{:S(2)}, u32[]{:S(2)}) collective-permute-start(bf16[2,100,1024]{2,1,0:T(8,128)(2,1)S(1)} %get-tuple-element.42), channel_id=1, source_target_pairs={{0,1},{1,0},{2,3},{3,2},{4,5},{5,4},{6,7},{7,6},{8,9},{9,8},{10,11... | collective-permute-start | bytes 1228808 | tf_op jit(solution)/shard_map/ppermute | solution.py:330
  775.9 12.7 %copy-start.2 = (bf16[2,2,2,2,2,2,32,3200]{7,6,5,4,3,2,1,0:T(8,128)(2,1)S(1)}, bf16[2,2,2,2,2,2,32,3200]{7,6,5,4,3,2,1,0:T(8,128)(2,1)}, u32[]{:S(2)}) copy-start(bf16[2,2,2,2,2,2,32,3200]{7,6,5,4,3,2,1,0:T(8,128)(2,1)} %get-tuple-element.25) | copy-start | bytes 39321604
  775.9 19.4 %slice-start = ((s8[13107200]{0:T(1024)(128)(4,1)}), s8[4194304]{0:T(1024)(128)(4,1)S(1)}, s32[]{:S(2)}) async-start(s8[13107200]{0:T(1024)(128)(4,1)} %bitcast.93), calls=%async_computation | async-start | bytes 8388608
  775.9 20.5 %slice-start.1 = ((s8[13107200]{0:T(1024)(128)(4,1)}), s8[4194304]{0:T(1024)(128)(4,1)S(1)}, s32[]{:S(2)}) async-start(s8[13107200]{0:T(1024)(128)(4,1)} %bitcast.93), calls=%async_computation.1 | async-start | bytes 8388608
  788.6 9.1 %slice-start.2 = ((s8[13107200]{0:T(1024)(128)(4,1)}), s8[4194304]{0:T(1024)(128)(4,1)S(1)}, s32[]{:S(2)}) async-start(s8[13107200]{0:T(1024)(128)(4,1)} %bitcast.93), calls=%async_computation.2 | async-start | bytes 8388608
  788.6 9.1 %slice-start.3 = ((s8[13107200]{0:T(1024)(128)(4,1)}), s8[524288]{0:T(1024)(128)(4,1)S(1)}, s32[]{:S(2)}) async-start(s8[13107200]{0:T(1024)(128)(4,1)} %bitcast.93), calls=%async_computation.3 | async-start | bytes 1048576

commit v2 on v1

--- a/solution.py
+++ b/solution.py
@@ -93,7 +93,11 @@
     grads, outs, refs = refs[:n], refs[n : 2 * n], refs[2 * n :]
     totals, firsts, refs = refs[:n], refs[n : 2 * n], refs[2 * n :]
     gots, refs = [refs[12 * u : 12 * u + 12] for u in range(n)], refs[12 * n :]
-    last, send, recv, local = refs
+    lasts = {}
+    for u in range(n):
+        if kinds[u] == "d":
+            lasts[u], refs = refs[0], refs[1:]
+    send, recv, local = refs
     bits, partners = place()
     core = bits[CORE]
     greet(partners)
@@ -161,21 +165,21 @@
                         continue
                     (rows, columns), _ = part_of(kinds[u], color)
                     if kinds[u] == "d":
-                        last[rows, pl.ds(pl.multiple_of(core * 512, 512), 512)] = total(u, color, bits[:4], 4)
+                        lasts[u][rows, pl.ds(pl.multiple_of(core * 512, 512), 512)] = total(u, color, bits[:4], 4)
                     else:
                         outs[u][rows, columns] = total(u, color, bits[:4], 4)
                 if s == 4:
                     if kinds[u] == "d":
                         columns = (slice(None), pl.ds(pl.multiple_of(core * 512, 512), 512))
-                        copy = remote(last.at[columns], last.at[columns], send.at[u, 13], recv.at[u, 13], partners[CORE])
+                        copy = remote(lasts[u].at[columns], lasts[u].at[columns], send.at[u, 13], recv.at[u, 13], partners[CORE])
                         copy.start()
-                        flying["d"] = copy
+                        flying["d", u] = copy
     for u in range(n):
         if kinds[u] == "d":
-            copy = flying["d"]
+            copy = flying["d", u]
             copy.wait_recv()
             waits.append(copy)
-            outs[u][...] = last[...]
+            outs[u][...] = lasts[u][...]
     for copy in waits:
         copy.wait_send()
 
@@ -188,32 +192,32 @@
         for color in range(3):
             for s in range(4):
                 scratch.append(pltpu.VMEM((2,) * (3 - s) + part_of(k, color)[1], BF16))
-    scratch += [pltpu.VMEM((200, 1024), BF16), pltpu.SemaphoreType.DMA((n, 14)), pltpu.SemaphoreType.DMA((n, 14)), pltpu.SemaphoreType.DMA((n,))]
+    scratch += [pltpu.VMEM((200, 1024), BF16)] * kinds.count("d")
+    scratch += [pltpu.SemaphoreType.DMA((n, 14)), pltpu.SemaphoreType.DMA((n, 14)), pltpu.SemaphoreType.DMA((n,))]
     return pl.pallas_call(
         functools.partial(reduce_kernel, kinds),
         out_shape=[jax.ShapeDtypeStruct((200, 1024) if k == "d" else (32, 3200), BF16) for k in kinds],
         in_specs=[pl.BlockSpec(memory_space=pltpu.HBM)] * n,
         out_specs=[pl.BlockSpec(memory_space=pltpu.VMEM)] * n,
         scratch_shapes=scratch,
-        compiler_params=pltpu.CompilerParams(collective_id=collective_id, has_side_effects=True, vmem_limit_bytes=60 * 2**20),
+        compiler_params=pltpu.CompilerParams(collective_id=collective_id, has_side_effects=True, vmem_limit_bytes=62 * 2**20),
         name=f"reduce_{collective_id}",
     )(*grads)
 
 
-def gather_kernel(units, *refs):
-    n = len(units)
-    blocks, outs, (send, recv, local) = refs[:n], refs[n : n + 3], refs[n + 3 :]
+def gather_kernel(kinds, *refs):
+    n = len(kinds)
+    blocks, outs, (send, recv, local) = refs[:n], refs[n : 2 * n], refs[2 * n :]
     bits, partners = place()
     core = bits[CORE]
     greet(partners)
 
     def at(u, index, color):
-        kind, layer = units[u]
-        (rows, columns), _ = part_of(kind, color)
-        out = outs[KINDS.index(kind)]
-        if kind == "d":
-            return out.at[(layer, *window(index), rows, pl.ds(pl.multiple_of(core * 512, 512), 512))]
-        return out.at[(layer, *window(index), core, rows, columns)]
+        (rows, columns), _ = part_of(kinds[u], color)
+        out = outs[u]
+        if kinds[u] == "d":
+            return out.at[(*window(index), rows, pl.ds(pl.multiple_of(core * 512, 512), 512))]
+        return out.at[(*window(index), core, rows, columns)]
 
     sent = []
     flying = {}
@@ -236,10 +240,9 @@
         for u in reversed(range(n)):
             s = t - u
             if s == 0:
-                kind, layer = units[u]
                 for color in range(3):
                     state[u, color] = list(bits[:4])
-                    (rows, columns), _ = part_of(kind, color)
+                    (rows, columns), _ = part_of(kinds[u], color)
                     src = blocks[u].at[rows, columns]
                     launch(u, color, 0, src)
                     across(u, color, src, state[u, color], 4)
@@ -266,14 +269,14 @@
             copy.wait_recv()
 
 
-def all_gather(blocks, units, layers, collective_id):
-    n = len(units)
-    shapes = [(layers, 2, 2, 2, 2, 200, 1024)] + [(layers, 2, 2, 2, 2, 2, 32, 3200)] * 2
+def all_gather(blocks, kinds, collective_id):
+    n = len(kinds)
+    shapes = [(2, 2, 2, 2, 200, 1024) if k == "d" else (2, 2, 2, 2, 2, 32, 3200) for k in kinds]
     return pl.pallas_call(
-        functools.partial(gather_kernel, units),
+        functools.partial(gather_kernel, kinds),
         out_shape=[jax.ShapeDtypeStruct(s, BF16) for s in shapes],
         in_specs=[pl.BlockSpec(memory_space=pltpu.VMEM)] * n,
-        out_specs=[pl.BlockSpec(memory_space=pltpu.HBM)] * 3,
+        out_specs=[pl.BlockSpec(memory_space=pltpu.HBM)] * n,
         scratch_shapes=[pltpu.SemaphoreType.DMA((n, 27)), pltpu.SemaphoreType.DMA((n, 27)), pltpu.SemaphoreType.DMA((n, 3))],
         compiler_params=pltpu.CompilerParams(collective_id=collective_id, has_side_effects=True),
         name=f"gather_{collective_id}",
@@ -298,43 +301,61 @@
             saved.append((h, a, scale, gate, up, act))
             if i + 1 < layers:
                 h = h + dot(act, wd[i], 1, 0).astype(BF16)
+        def rows_of(t, kind):
+            rows = old[kind][1].shape[1]
+            return lax.dynamic_slice_in_dim(t, me * rows, rows, 0)
+
+        def update(kind, i, g):
+            w, m, v = (t[i] for t in old[kind])
+            return adamw(rows_of(w, kind).astype(F32), m, v, g.astype(F32))
+
+        def by_chips(t, kind):
+            return t.reshape(2, 2, 2, 2, 200, 1024) if kind == "d" else t.reshape(2, 2, 2, 2, 2, 32, 3200)
+
         d = dy
-        summed = {}
+        grads, new, full = {}, {}, {}
         for i in reversed(range(layers)):
             h, a, scale, gate, up, act = saved[i]
-            by_d = dot(act, d, 0, 0).astype(BF16)
             d_act = dot(d, wd[i], 1, 1).astype(BF16).astype(F32)
             sig = jax.nn.sigmoid(gate)
             d_up = (d_act * (gate * sig)).astype(BF16)
             d_gate = (d_act * up * (sig * (1 + gate * (1 - sig)))).astype(BF16)
-            by_g = dot(a, d_gate, 0, 0).astype(BF16)
-            by_u = dot(a, d_up, 0, 0).astype(BF16)
-            grads = [by_d.reshape(2, 2, 2, 2, 200, 1024)] + [t.reshape(2, 2, 2, 2, 2, 32, 3200) for t in (by_g, by_u)]
-            summed[i] = dict(zip(KINDS, reduce_scatter(grads, KINDS, i)))
+            grads["g", i] = dot(a, d_gate, 0, 0).astype(BF16)
+            if i:
+                early = lax.psum_scatter(grads.pop(("g", i)).reshape(32, 32, 3200), "dp", scatter_dimension=0, tiled=True)
+            grads["d", i] = dot(act, d, 0, 0).astype(BF16)
+            if not i:
+                early, grads["g", 0], grads["d", 0] = lax.optimization_barrier((early, grads["g", 0], grads["d", 0]))
+                new["g", 1] = update("g", 1, early[0])
+                block, d_up = lax.optimization_barrier((new["g", 1][0], d_up))
+                full["g", 1] = lax.all_gather(block, "dp", axis=0, tiled=True)
+            grads["u", i] = dot(a, d_up, 0, 0).astype(BF16)
             if i:
                 da = dot(d_gate, wg[i], 1, 1).astype(BF16) + dot(d_up, wu[i], 1, 1).astype(BF16)
                 da = da.astype(F32)
                 wide = h.astype(F32)
                 inner = jnp.mean(da * wide, -1, keepdims=True)
                 d = d + (scale * da - wide * (scale**3 * inner)).astype(BF16)
-        new = {}
-        for kind in KINDS:
-            w, m, v = old[kind]
-            rows = m.shape[1]
-            g = jnp.stack([summed[i][kind] for i in range(layers)])
+        units = [("u", 1), ("d", 1), ("g", 0), ("u", 0), ("d", 0)]
+        kinds = tuple(k for k, _ in units)
+        summed = dict(zip(units, reduce_scatter([by_chips(grads[u], u[0]) for u in units], kinds, 0)))
+        for kind, i in units:
+            g = summed[kind, i]
             if kind == "d":
-                g = lax.dynamic_slice_in_dim(g, core * rows, rows, 1)
-            mine = lax.dynamic_slice_in_dim(w, me * rows, rows, 1)
-            new[kind] = adamw(mine.astype(F32), m, v, g.astype(F32))
-        mine = new["d"][0]
+                g = lax.dynamic_slice_in_dim(g, core * 100, 100, 0)
+            new[kind, i] = update(kind, i, g)
+        mine = jnp.stack([new["d", i][0] for i in range(layers)])
         other = lax.ppermute(mine, "dp", [(k, k + 1 - 2 * (k % 2)) for k in range(32)])
         first = core == 0
         whole = jnp.concatenate([jnp.where(first, mine, other), jnp.where(first, other, mine)], 1)
-        part = {"d": lax.dynamic_slice_in_dim(whole, core * 512, 512, 2), "g": new["g"][0], "u": new["u"][0]}
-        units = tuple((kind, i) for i in reversed(range(layers)) for kind in KINDS)
-        full = all_gather([part[kind][i] for kind, i in units], units, layers, 2)
-        full = {kind: t.reshape(old[kind][0].shape) for kind, t in zip(KINDS, full)}
-        return tuple(full[k] for k in "gud") + tuple(new[k][1] for k in "gud") + tuple(new[k][2] for k in "gud")
+        part = lax.dynamic_slice_in_dim(whole, core * 512, 512, 2)
+        blocks = [part[i] if kind == "d" else new[kind, i][0] for kind, i in units]
+        for (kind, i), t in zip(units, all_gather(blocks, kinds, 1)):
+            full[kind, i] = t.reshape(old[kind][0].shape[1:])
+        outs = [jnp.stack([full[k, i] for i in range(layers)]) for k in "gud"]
+        for which in (1, 2):
+            outs += [jnp.stack([new[k, i][which] for i in range(layers)]) for k in "gud"]
+        return tuple(outs)
 
     seq, whole, rows = P(("rep", "dp")), P(), P(None, "dp")
     return jax.shard_map(

time: 810 us -> 794 us (0.980)
  Pallas kernels: 371 us -> 310 us
  other arithmetic: 15.8 us -> 47.7 us
  between operations: 1.25 us -> 14.8 us
    pallas_call x2 -> x1, Pallas kernels: 199 us -> 160 us  [reduce_scatter(): pl.pallas_call(functools.partial(reduce_kernel, kinds), out_shape=[jax.Sh...]
    slice x0 -> x5, local copies, waits for them, and re-layouts: none -> 34.5 us  [the longest x1 10.8 us: local(): h = h + dot(act, wd[i], 1, 0).astype(BF16)]
    another operation x0 -> x11, other arithmetic: none -> 34.4 us  [the longest x3 27.9 us: local(): outs = [jnp.stack([full[k, i] for i in range(layers)]) for k in 'gud']]
    unnamed x41 -> x52, local copies, waits for them, and re-layouts: 44.8 us -> 17.8 us
    pallas_call x1, Pallas kernels: 172 us -> 150 us  [all_gather(): pl.pallas_call(functools.partial(gather_kernel, kinds), out_shape=[jax.Sh...]
  transfers between devices with their start and end apart: 1 -> 3, of which waited for: 0 -> 0; matrix products, arithmetic and copies ran while one was open for 1% -> 33% of each run, Pallas kernels for 0% -> 39%
where the time goes in v2:
time: 794 us; the launch traced here: 788 us
  matrix products  361 us (45%)
  Pallas kernels  310 us (39%)
  local copies, waits for them, and re-layouts  53.1 us (7%)
  other arithmetic  47.7 us (6%)
  between operations  14.8 us (2%)
    dot_general x15, matrix products, dot(): lax.dot_general(a, b, (((ca,), (cb,)), ((), ())), preferred_element_type=...  361 us
    pallas_call x1, Pallas kernels, reduce_scatter(): pl.pallas_call(functools.partial(reduce_kernel, kinds), out_shape=[jax.Sh...  160 us
    pallas_call x1, Pallas kernels, all_gather(): pl.pallas_call(functools.partial(gather_kernel, kinds), out_shape=[jax.Sh...  150 us
    another operation x3, other arithmetic, local(): outs = [jnp.stack([full[k, i] for i in range(layers)]) for k in 'gud']  27.9 us
    unnamed x52, local copies, waits for them, and re-layouts  17.8 us
  transfers between devices with their start and end apart: 3, of which 0 were waited for; matrix products, arithmetic and copies ran while one was open for 33% of the time, Pallas kernels for 39%

profile of v2, /device:TPU:0, one launch (start us, length us, event | category | flops | bytes accessed | tf_op | source)
XLA Modules:
  0.0 787.5 jit_solution(659263088847393275)
XLA Ops:
  7.2 0.0 reduce-scatter.2.cloned.1.call-start
  7.2 6.5 copy.20
  13.7 3.1 fusion.11
  16.8 21.9 %fusion.36 = f32[2048,3200]{1,0:T(8,128)} fusion(bf16[1,2048,1024]{2,1,0:T(8,128)(2,1)} %param.11, f32[2048]{0:T(1024)S(1)} %add_rsqrt_fusion.1, bf16[2,1024,3200]{2,1,0:T(8,128)(2,1)} %param.13), kind=kOutput, calls=%fused_computation.58 | convolution fusion | flops 13428064256 | bytes 36970496 | tf_op jit(solution)/shard_map/dot_general | solution.py:23
  38.7 32.1 %multiply_convert_fusion.1 = (bf16[2048,3200]{1,0:T(8,128)(2,1)}, f32[2048,3200]{1,0:T(8,128)}) fusion(f32[2048,3200]{1,0:T(8,128)} %fusion.36, bf16[2,1024,3200]{2,1,0:T(8,128)(2,1)} %param.14, bf16[1,2048,1024]{2,1,0:T(8,128)(2,1)} %param.11, f32[2048]{0:T(1024)S(1)} %add_rsqrt_fusion.1), kind=kOutput, calls=%fused_computation.13 | convolution fusion | flops 13467385856 | bytes 76292096 | tf_op jit(solution)/shard_map/dot_general | solution.py:23
  70.8 22.4 %fusion.15 = (f32[2048]{0:T(1024)S(1)}, bf16[2048,1024]{0,1:T(8,128)(2,1)}) fusion(bf16[2048,3200]{1,0:T(8,128)(2,1)} %get-tuple-element.81, bf16[2,3200,1024]{2,1,0:T(8,128)(2,1)} %param.15, bf16[1,2048,1024]{1,2,0:T(8,128)(2,1)} %copy.20), kind=kOutput, calls=%fused_computation.34 | convolution fusion | flops 13432256512 | bytes 28057600 | tf_op jit(solution)/shard_map/dot_general | solution.py:23
  93.2 0.0 copy-start.17
  93.2 0.6 copy-done.19
  93.8 23.1 %fusion.28 = f32[2048,3200]{1,0:T(8,128)} fusion(bf16[2048,1024]{0,1:T(8,128)(2,1)} %get-tuple-element.84, f32[2048]{0:T(1024)S(1)} %add_rsqrt_fusion, bf16[2,1024,3200]{2,1,0:T(8,128)(2,1)} %param.13), kind=kOutput, calls=%fused_computation.50 | convolution fusion | flops 13428064256 | bytes 36970496 | tf_op jit(solution)/shard_map/dot_general | solution.py:23
  116.9 20.9 %fusion.24 = f32[2048,3200]{1,0:T(8,128)} fusion(bf16[2048,1024]{0,1:T(8,128)(2,1)S(1)} %copy-done.4, f32[2048]{0:T(1024)S(1)} %add_rsqrt_fusion, bf16[2,1024,3200]{2,1,0:T(8,128)(2,1)} %param.14), kind=kOutput, calls=%fused_computation.46 | convolution fusion | flops 13428064256 | bytes 36970496 | tf_op jit(solution)/shard_map/dot_general | solution.py:23
  137.7 0.0 copy-done.6
  137.7 35.1 %fusion = (bf16[2048,3200]{1,0:T(8,128)(2,1)}, bf16[2048,3200]{1,0:T(8,128)(2,1)}) fusion(f32[2048,3200]{1,0:T(8,128)} %fusion.28, f32[2048,3200]{1,0:T(8,128)} %fusion.24, bf16[2,3200,1024]{2,1,0:T(8,128)(2,1)} %param.15, bf16[1,2048,1024]{2,1,0:T(8,128)(2,1)S(1)} %copy-done.6), kind=kOutput, calls=%fused_computation.4 | convolution fusion | flops 13520076800 | bytes 89391104 | tf_op jit(solution)/shard_map/dot_general | solution.py:23
  172.8 20.4 %convolution_convert_fusion.4 = bf16[1024,3200]{1,0:T(8,128)(2,1)} fusion(bf16[2048,3200]{1,0:T(8,128)(2,1)} %get-tuple-element.49, bf16[2048,1024]{0,1:T(8,128)(2,1)S(1)} %copy-done.4, f32[2048]{0:T(1024)S(1)} %add_rsqrt_fusion), kind=kOutput, calls=%fused_computation.42 | convolution fusion | flops 13431341056 | bytes 23863296 | tf_op jit(solution)/shard_map/dot_general | solution.py:23
  193.2 0.0 reduce-scatter.2.cloned.1.call-update
  193.3 0.0 all-gather.2.cloned.1.call-start
  193.3 6.8 copy.21
  200.1 10.3 %fusion.123 = (bf16[1,1024,3200]{2,1,0:T(8,128)(2,1)}, bf16[1,1024,3200]{2,1,0:T(8,128)(2,1)}) fusion(bf16[2,1024,3200]{2,1,0:T(8,128)(2,1)} %param.13), kind=kLoop, calls=%fused_computation.182 | loop fusion | bytes 26214400 | tf_op jit(solution)/shard_map/slice | solution.py:298
  210.5 25.7 %fusion.21 = bf16[3200,1024]{1,0:T(8,128)(2,1)} fusion(f32[2048,3200]{1,0:T(8,128)} %fusion.24, f32[2048,3200]{1,0:T(8,128)} %fusion.28, bf16[1,2048,1024]{2,1,0:T(8,128)(2,1)} %param.12), kind=kOutput, calls=%fused_computation.39 | convolution fusion | flops 13464371200 | bytes 63176704 | tf_op jit(solution)/shard_map/dot_general | solution.py:23
  236.2 10.3 %fusion.122 = (bf16[1,1024,3200]{2,1,0:T(8,128)(2,1)}, bf16[1,1024,3200]{2,1,0:T(8,128)(2,1)}) fusion(bf16[2,1024,3200]{2,1,0:T(8,128)(2,1)} %param.14), kind=kLoop, calls=%fused_computation.181 | loop fusion | bytes 26214400 | tf_op jit(solution)/shard_map/slice | solution.py:299
  246.5 10.8 %fusion.124 = (bf16[1,3200,1024]{2,1,0:T(8,128)(2,1)}, bf16[1,3200,1024]{2,1,0:T(8,128)(2,1)}) fusion(bf16[2,3200,1024]{2,1,0:T(8,128)(2,1)} %param.15), kind=kLoop, calls=%fused_computation.183 | loop fusion | bytes 26214400 | tf_op jit(solution)/shard_map/slice | solution.py:303
  257.3 19.8 %fusion.22 = bf16[2048,1024]{0,1:T(8,128)(2,1)} fusion(bf16[2048,3200]{1,0:T(8,128)(2,1)} %get-tuple-element.48, bf16[2,1024,3200]{2,1,0:T(8,128)(2,1)} %param.14), kind=kOutput, calls=%fused_computation.44 | convolution fusion | flops 13421772800 | bytes 23855104 | tf_op jit(solution)/shard_map/dot_general | solution.py:23
  277.1 23.4 %fusion.17 = (f32[2048]{0:T(1024)S(1)}, bf16[2048,1024]{0,1:T(8,128)(2,1)}) fusion(bf16[2048,1024]{0,1:T(8,128)(2,1)} %get-tuple-element.84, bf16[2048,1024]{0,1:T(8,128)(2,1)} %fusion.22, bf16[2048,3200]{1,0:T(8,128)(2,1)} %get-tuple-element.49, bf16[2,1024,3200]{2,1,0:T(8,128)(2,1)} %param.13), kind=kOutput, calls=%fused_computation.36 | convolution fusion | flops 13434353664 | bytes 32251904 | tf_op jit(solution)/shard_map/dot_general | solution.py:23
  300.5 5.3 fusion.40
  305.8 0.0 copy-start.9
  305.8 0.0 copy-start.10
  305.9 21.0 %convolution_convert_fusion.3 = bf16[3200,1024]{1,0:T(8,128)(2,1)} fusion(bf16[2048,3200]{1,0:T(8,128)(2,1)} %get-tuple-element.81, bf16[2048,1024]{0,1:T(8,128)(2,1)S(1)} %fusion.40), kind=kOutput, calls=%fused_computation.41 | convolution fusion | flops 13425049600 | bytes 23855104 | tf_op jit(solution)/shard_map/dot_general | solution.py:23
  326.9 0.0 copy-done.9
  326.9 1.5 fusion.126
  328.4 1.5 fusion.125
  329.9 26.9 %fusion.5 = (bf16[2048,3200]{1,0:T(8,128)(2,1)}, bf16[2048,3200]{1,0:T(8,128)(2,1)}) fusion(f32[2048,3200]{1,0:T(8,128)} %fusion.36, bf16[2048,1024]{0,1:T(8,128)(2,1)} %copy-done.5, bf16[2,3200,1024]{2,1,0:T(8,128)(2,1)} %param.15), kind=kOutput, calls=%fused_computation.9 | convolution fusion | flops 13474201600 | bytes 63176704 | tf_op jit(solution)/shard_map/dot_general | solution.py:23
  356.8 0.0 copy-done.22
  356.8 0.0 copy-start.8
  356.8 0.0 copy-start.18
  356.8 31.4 %fusion.18 = bf16[1024,3200]{1,0:T(8,128)(2,1)} fusion(f32[2048,3200]{1,0:T(8,128)} %get-tuple-element.82, bf16[2048,3200]{1,0:T(8,128)(2,1)} %get-tuple-element.88, f32[2048,3200]{1,0:T(8,128)} %fusion.36, bf16[1,2048,1024]{1,2,0:T(8,128)(2,1)} %copy.20, f32[2048]{0:T(1024)S(1)} %copy-done.22), kind=kOutput, calls=%fused_computation.38 | convolution fusion | flops 13503430656 | bytes 76292096 | tf_op jit(solution)/shard_map/dot_general | solution.py:23
  388.2 0.0 copy-done.7
  388.2 2.0 fusion.77
  390.2 0.0 all-gather.2.cloned.1.call-update
  390.2 0.0 copy-start.23
  390.2 21.2 %convolution_convert_fusion.5 = bf16[1024,3200]{1,0:T(8,128)(2,1)} fusion(bf16[2048,3200]{1,0:T(8,128)(2,1)} %get-tuple-element.48, bf16[2048,1024]{0,1:T(8,128)(2,1)} %get-tuple-element.84, f32[2048]{0:T(1024)S(1)} %copy-done.18), kind=kOutput, calls=%fused_computation.43 | convolution fusion | flops 13431341056 | bytes 23863296 | tf_op jit(solution)/shard_map/dot_general | solution.py:23
  411.4 16.3 %convolution_convert_fusion.2 = bf16[1024,3200]{1,0:T(8,128)(2,1)} fusion(bf16[2048,3200]{1,0:T(8,128)(2,1)S(1)} %copy-done.23, bf16[1,2048,1024]{1,2,0:T(8,128)(2,1)S(1)} %copy-done.1, f32[2048]{0:T(1024)S(1)} %copy-done.22), kind=kOutput, calls=%fused_computation.40 | convolution fusion | flops 13431341056 | bytes 23863296 | tf_op jit(solution)/shard_map/dot_general | solution.py:23
  427.7 159.9 %reduce_0.1 = (bf16[32,3200]{1,0:T(8,128)(2,1)}, bf16[200,1024]{1,0:T(8,128)(2,1)}, bf16[32,3200]{1,0:T(8,128)(2,1)}, bf16[32,3200]{1,0:T(8,128)(2,1)}, bf16[200,1024]{1,0:T(8,128)(2,1)}) custom-call(bf16[2,2,2,2,2,32,3200]{6,5,4,3,2,1,0:T(8,128)(2,1)} %bitcast.245, bf16[2,2,2,2,200,1024]{5,4,3,2,1,0:T(8,128)(2,1)} %bitcast.242, ...), custom_call_target="tpu_custom_call" | custom-call | tf_op jit(solution)/shard_map/reduce_0/pallas_call | solution.py:197
  587.7 0.0 copy-start.12
  587.7 0.0 copy-start.13
  587.7 2.5 fusion.100
  590.3 0.6 collective-permute-start
  590.9 0.1 pad_maximum_fusion.3
  590.9 1.5 copy.26
  592.5 0.1 pad_maximum_fusion.4
  592.5 1.5 copy.27
  594.0 0.1 fusion.96
  594.2 2.6 fusion.86
  596.8 0.9 pad_maximum_fusion.5
  597.7 0.9 pad_maximum_fusion.6
  598.7 0.9 pad_maximum_fusion.7
  599.6 0.9 pad_maximum_fusion.8
  600.6 0.0 collective-permute-done
  600.6 0.1 broadcast_select_fusion
  600.6 0.2 fusion.97
  600.8 0.8 slice_bitcast_fusion
  601.6 150.0 %gather_1.1 = (bf16[2,2,2,2,2,32,3200]{6,5,4,3,2,1,0:T(8,128)(2,1)}, bf16[2,2,2,2,200,1024]{5,4,3,2,1,0:T(8,128)(2,1)}, bf16[2,2,2,2,2,32,3200]{6,5,4,3,2,1,0:T(...) custom-call(bf16[32,3200]{1,0:T(8,128)(2,1)} %get-tuple-element.57.refs_0_, ...), custom_call_target="tpu_custom_call" | custom-call | tf_op jit(solution)/shard_map/gather_1/pallas_call | solution.py:275
  751.6 12.7 %pad_maximum_fusion.1 = bf16[2,1024,3200]{2,1,0:T(8,128)(2,1)} fusion(bf16[1,1024,3200]{2,1,0:T(8,128)(2,1)} %bitcast.240, bf16[1,1024,3200]{2,1,0:T(8,128)(2,1)} %bitcast.241), kind=kLoop, calls=%fused_computation.24 | loop fusion | flops 6553600 | bytes 26214400 | tf_op jit(solution)/shard_map/stack | solution.py:355
  764.3 0.7 copy-done.3
  765.0 5.3 pad_maximum_fusion.2
  770.3 9.9 %pad_maximum_fusion = bf16[2,1024,3200]{2,1,0:T(8,128)(2,1)} fusion(bf16[1,1024,3200]{2,1,0:T(8,128)(2,1)} %bitcast.235, bf16[1,1024,3200]{2,1,0:T(8,128)(2,1)} %bitcast.237), kind=kLoop, calls=%fused_computation.23 | loop fusion | flops 6553600 | bytes 26214400 | tf_op jit(solution)/shard_map/stack | solution.py:355
  (40 shorter events, 0.1 us)
Async XLA Ops:
  7.2 381.0 %reduce-scatter.2.cloned.1.call-start = ((), (), s32[]{:S(2)}) async-start(), calls=%async_computation.1 | async-start | bytes 6758400 | tf_op jit(solution)/shard_map/reduce_scatter | solution.py:325
  16.8 21.9 %copy-start.21 = (f32[2048]{0:T(1024)}, f32[2048]{0:T(1024)S(1)}, u32[]{:S(2)}) copy-start(f32[2048]{0:T(1024)S(1)} %add_rsqrt_fusion.1) | copy-start | bytes 24580
  93.2 0.6 copy-start.19
  93.2 207.3 %copy-start.17 = (f32[2048]{0:T(1024)}, f32[2048]{0:T(1024)S(1)}, u32[]{:S(2)}) copy-start(f32[2048]{0:T(1024)S(1)} %add_rsqrt_fusion) | copy-start | bytes 24580
  93.8 23.1 %copy-start.4 = (bf16[2048,1024]{0,1:T(8,128)(2,1)S(1)}, bf16[2048,1024]{0,1:T(8,128)(2,1)}, u32[]{:S(2)}) copy-start(bf16[2048,1024]{0,1:T(8,128)(2,1)} %get-tuple-element.84) | copy-start | bytes 12582916
  116.9 20.9 %copy-start.6 = (bf16[1,2048,1024]{2,1,0:T(8,128)(2,1)S(1)}, bf16[1,2048,1024]{2,1,0:T(8,128)(2,1)}, u32[]{:S(2)}) copy-start(bf16[1,2048,1024]{2,1,0:T(8,128)(2,1)} %param.12) | copy-start | bytes 12582916
  193.3 577.1 %all-gather.2.cloned.1.call-start = ((), (), s32[]{:S(2)}) async-start(), calls=%async_computation.2 | async-start | bytes 6758400 | tf_op jit(solution)/shard_map/all_gather | solution.py:331
  277.1 23.4 %copy-start.20 = (f32[2048]{0:T(1024)S(1)}, f32[2048]{0:T(1024)}, u32[]{:S(2)}) copy-start(f32[2048]{0:T(1024)} %copy-done.19) | copy-start | bytes 24580
  277.1 23.4 %copy-start = (bf16[1,2048,1024]{1,2,0:T(8,128)(2,1)S(1)}, bf16[1,2048,1024]{1,2,0:T(8,128)(2,1)}, u32[]{:S(2)}) copy-start(bf16[1,2048,1024]{1,2,0:T(8,128)(2,1)} %copy.21) | copy-start | bytes 12582916
  305.8 21.1 %copy-start.5 = (bf16[2048,1024]{0,1:T(8,128)(2,1)}, bf16[2048,1024]{0,1:T(8,128)(2,1)S(1)}, u32[]{:S(2)}) copy-start(bf16[2048,1024]{0,1:T(8,128)(2,1)S(1)} %fusion.40) | copy-start | bytes 12582916
  305.8 21.1 %copy-start.9 = (f32[2,100,1024]{2,0,1:T(2,128)S(1)}, f32[2,100,1024]{2,0,1:T(2,128)}, u32[]{:S(2)}) copy-start(f32[2,100,1024]{2,0,1:T(2,128)} %param.21) | copy-start | bytes 2457604
  305.8 22.6 %copy-start.10 = (f32[2,100,1024]{2,0,1:T(2,128)S(1)}, f32[2,100,1024]{2,0,1:T(2,128)}, u32[]{:S(2)}) copy-start(f32[2,100,1024]{2,0,1:T(2,128)} %param.18) | copy-start | bytes 2457604
  329.9 26.9 %copy-start.22 = (f32[2048]{0:T(1024)S(1)}, f32[2048]{0:T(1024)}, u32[]{:S(2)}) copy-start(f32[2048]{0:T(1024)} %copy-done.21) | copy-start | bytes 24580
  356.8 31.4 %copy-start.7 = (f32[2,32,3200]{2,1,0:T(8,128)S(1)}, f32[2,32,3200]{2,1,0:T(8,128)}, u32[]{:S(2)}) copy-start(f32[2,32,3200]{2,1,0:T(8,128)} %param.16) | copy-start | bytes 2457604
  356.8 31.4 %copy-start.8 = (f32[2,32,3200]{2,1,0:T(8,128)S(1)}, f32[2,32,3200]{2,1,0:T(8,128)}, u32[]{:S(2)}) copy-start(f32[2,32,3200]{2,1,0:T(8,128)} %param.19) | copy-start | bytes 2457604
  356.8 33.4 %copy-start.18 = (f32[2048]{0:T(1024)S(1)}, f32[2048]{0:T(1024)}, u32[]{:S(2)}) copy-start(f32[2048]{0:T(1024)} %copy-done.17) | copy-start | bytes 24580
  390.2 21.2 %copy-start.1 = (bf16[1,2048,1024]{1,2,0:T(8,128)(2,1)S(1)}, bf16[1,2048,1024]{1,2,0:T(8,128)(2,1)}, u32[]{:S(2)}) copy-start(bf16[1,2048,1024]{1,2,0:T(8,128)(2,1)} %copy.20) | copy-start | bytes 12582916
  390.2 21.2 %copy-start.23 = (bf16[2048,3200]{1,0:T(8,128)(2,1)S(1)}, bf16[2048,3200]{1,0:T(8,128)(2,1)}, u32[]{:S(2)}) copy-start(bf16[2048,3200]{1,0:T(8,128)(2,1)} %get-tuple-element.26) | copy-start | bytes 39321604
  587.7 6.4 copy-start.11
  587.7 6.5 copy-start.12
  587.7 6.5 copy-start.13
  587.7 6.5 copy-start.14
  587.7 6.5 copy-start.15
  587.7 6.5 copy-start.16
  590.3 10.2 %collective-permute-start = (bf16[2,100,1024]{2,1,0:T(8,128)(2,1)S(1)}, bf16[2,100,1024]{2,1,0:T(8,128)(2,1)S(1)}, u32[]{:S(2)}, u32[]{:S(2)}) collective-permute-start(bf16[2,100,1024]{2,1,0:T(8,128)(2,1)S(1)} %pad_maximum_fusion.9), channel_id=1, source_target_pairs={{0,1},{1,0},{2,3},{3,2},{4,5},{5,4},{6,7},{7,6},{8,9},{9,8},{10,11... | collective-permute-start | bytes 1228808 | tf_op jit(solution)/shard_map/ppermute | solution.py:348
  751.6 12.7 %copy-start.2 = (bf16[2,2,2,2,200,1024]{5,4,3,2,1,0:T(8,128)(2,1)S(1)}, bf16[2,2,2,2,200,1024]{5,4,3,2,1,0:T(8,128)(2,1)}, u32[]{:S(2)}) copy-start(bf16[2,2,2,2,200,1024]{5,4,3,2,1,0:T(8,128)(2,1)} %get-tuple-element.38) | copy-start | bytes 19660804
  751.6 13.4 %copy-start.3 = (bf16[2,2,2,2,200,1024]{5,4,3,2,1,0:T(8,128)(2,1)S(1)}, bf16[2,2,2,2,200,1024]{5,4,3,2,1,0:T(8,128)(2,1)}, u32[]{:S(2)}) copy-start(bf16[2,2,2,2,200,1024]{5,4,3,2,1,0:T(8,128)(2,1)} %get-tuple-element.37) | copy-start | bytes 19660804
Sparse Core Ops, SparseCore 0:
  193.4 149.5 reduce-scatter.1
  390.3 91.8 all-gather.1

commit v3 on v2

--- a/solution.py
+++ b/solution.py
@@ -88,18 +88,43 @@
     return tuple(slice(None) if i is None else i for i in index)
 
 
-def reduce_kernel(kinds, *refs):
-    n = len(kinds)
-    grads, outs, refs = refs[:n], refs[n : 2 * n], refs[2 * n :]
-    totals, firsts, refs = refs[:n], refs[n : 2 * n], refs[2 * n :]
-    gots, refs = [refs[12 * u : 12 * u + 12] for u in range(n)], refs[12 * n :]
-    lasts = {}
-    for u in range(n):
-        if kinds[u] == "d":
-            lasts[u], refs = refs[0], refs[1:]
-    send, recv, local = refs
+REDUCED = (("g", 1), ("u", 1), ("d", 1), ("d", 0), ("g", 0), ("u", 0))
+ROUND = (0, 1, 2, 3, 5, 6)
+SLOT = (0, 1, 2, 3, 0, 1)
+SLOT_KINDS = ("g", "u", "d", "d")
+COMPUTED = (1, 4, 5)
+WIDE = 640
+TILES = {0: range(0, 5), 1: range(5, 7), 2: range(7, 9), 3: range(9, 11), 4: range(11, 13), 5: range(13, 15)}
+
+
+def reduce_kernel(*refs):
+    n = len(REDUCED)
+    kinds = [k for k, _ in REDUCED]
+    given, refs = refs[:3], refs[3:]
+    lefts, rights, refs = refs[:2], refs[2:5], refs[5:]
+    outs, products, refs = refs[:n], refs[n : n + 3], refs[n + 3 :]
+    totals, firsts, refs = refs[:4], refs[4:8], refs[8:]
+    gots, refs = [refs[12 * i : 12 * i + 12] for i in range(4)], refs[48:]
+    lasts, refs = {2: refs[0], 3: refs[1]}, refs[2:]
+    lhs, rhs, tile, send, recv, local, free, lhs_sem, rhs_sem, tile_sem = refs
+    grads = {0: given[0], 2: given[1], 3: given[2], 1: products[0], 4: products[1], 5: products[2]}
     bits, partners = place()
     core = bits[CORE]
+
+    def load_lhs(layer):
+        return pltpu.make_async_copy(lefts[layer], lhs, lhs_sem)
+
+    def load_rhs(j):
+        columns = pl.ds(j % 5 * WIDE, WIDE)
+        return pltpu.make_async_copy(rights[j // 5].at[:, columns], rhs.at[j % 2], rhs_sem.at[j % 2])
+
+    def store(j):
+        columns = pl.ds(j % 5 * WIDE, WIDE)
+        out = products[j // 5].at[:, :, :, :, :, :, columns]
+        return pltpu.make_async_copy(tile.at[j % 2], out, tile_sem.at[j % 2])
+
+    load_lhs(1).start()
+    load_rhs(0).start()
     greet(partners)
 
     def halves(u, which):
@@ -107,23 +132,33 @@
             return grads[u].at[:, :, :, :, :, pl.ds(pl.multiple_of(which * 512, 512), 512)]
         return grads[u].at[:, :, :, :, which]
 
-    started = {}
-    for u in range(n):
-        copy = remote(halves(u, 1 - core), firsts[u], send.at[u, 12], recv.at[u, 12], partners[CORE])
+    started, waits, told = {}, {u: [] for u in range(n)}, set()
+
+    def may_write(u, dim):
+        if u >= 4 and (u, dim) not in told:
+            told.add((u, dim))
+            pl.semaphore_wait(free.at[u - 4, dim], 1)
+
+    def begin(u):
+        may_write(u, CORE)
+        copy = remote(halves(u, 1 - core), firsts[SLOT[u]], send.at[u, 12], recv.at[u, 12], partners[CORE])
         copy.start()
-        own = pltpu.make_async_copy(halves(u, core), totals[u], local.at[u])
+        own = pltpu.make_async_copy(halves(u, core), totals[SLOT[u]], local.at[u])
         own.start()
         started[u] = (copy, own)
 
+    for u in (0, 2, 3):
+        begin(u)
+
     state = {(u, color): [None] * 4 for u in range(n) for color in range(3)}
     flying = {}
 
     def total(u, color, at, steps):
         where = (*at, *part_of(kinds[u], color)[0])
-        value = totals[u][where].astype(F32) + firsts[u][where].astype(F32)
+        value = totals[SLOT[u]][where].astype(F32) + firsts[SLOT[u]][where].astype(F32)
         for s in range(steps):
             rest = tuple(at[i] for i in range(4) if i not in ORDERS[color][: s + 1])
-            got = gots[u][color * 4 + s]
+            got = gots[SLOT[u]][color * 4 + s]
             value += (got[rest] if rest else got[...]).astype(F32)
         return value.astype(BF16)
 
@@ -135,74 +170,116 @@
         k = color * 4 + s
 
         def ready(at):
-            totals[u][(*at, *part)] = total(u, color, at, s)
+            totals[SLOT[u]][(*at, *part)] = total(u, color, at, s)
 
         for_blocks(index, ready)
-        copy = remote(totals[u].at[(*window(index), *part)], gots[u][k], send.at[u, k], recv.at[u, k], partners[dim])
+        may_write(u, dim)
+        copy = remote(totals[SLOT[u]].at[(*window(index), *part)], gots[SLOT[u]][k], send.at[u, k], recv.at[u, k], partners[dim])
         copy.start()
         flying[u, color] = copy
         index[dim] = bits[dim]
         state[u, color] = index
 
-    waits = []
-    for t in range(n + 4):
-        for u in reversed(range(n)):
-            s = t - u
-            if s == 0:
-                copy, own = started[u]
-                own.wait()
-                copy.wait_recv()
-                waits.append(copy)
-                for color in range(3):
-                    launch(u, color, 0)
-            elif 0 < s <= 4:
-                for color in range(3):
-                    copy = flying[u, color]
-                    copy.wait_recv()
-                    waits.append(copy)
-                    if s < 4:
-                        launch(u, color, s)
-                        continue
-                    (rows, columns), _ = part_of(kinds[u], color)
-                    if kinds[u] == "d":
-                        lasts[u][rows, pl.ds(pl.multiple_of(core * 512, 512), 512)] = total(u, color, bits[:4], 4)
-                    else:
-                        outs[u][rows, columns] = total(u, color, bits[:4], 4)
-                if s == 4:
-                    if kinds[u] == "d":
-                        columns = (slice(None), pl.ds(pl.multiple_of(core * 512, 512), 512))
-                        copy = remote(lasts[u].at[columns], lasts[u].at[columns], send.at[u, 13], recv.at[u, 13], partners[CORE])
-                        copy.start()
-                        flying["d", u] = copy
-    for u in range(n):
-        if kinds[u] == "d":
-            copy = flying["d", u]
+    def step(u, s):
+        if s == 0:
+            copy, own = started[u]
+            own.wait()
             copy.wait_recv()
-            waits.append(copy)
-            outs[u][...] = lasts[u][...]
-    for copy in waits:
-        copy.wait_send()
-
-
-def reduce_scatter(grads, kinds, collective_id):
-    n = len(kinds)
+            waits[u].append(copy)
+            for color in range(3):
+                launch(u, color, 0)
+            return
+        for color in range(3):
+            copy = flying[u, color]
+            copy.wait_recv()
+            waits[u].append(copy)
+            if s < 4:
+                launch(u, color, s)
+                continue
+            (rows, columns), _ = part_of(kinds[u], color)
+            if kinds[u] == "d":
+                lasts[u][rows, pl.ds(pl.multiple_of(core * 512, 512), 512)] = total(u, color, bits[:4], 4)
+            else:
+                outs[u][rows, columns] = total(u, color, bits[:4], 4)
+        if s == 4:
+            if kinds[u] == "d":
+                columns = (slice(None), pl.ds(pl.multiple_of(core * 512, 512), 512))
+                copy = remote(lasts[u].at[columns], lasts[u].at[columns], send.at[u, 13], recv.at[u, 13], partners[CORE])
+                copy.start()
+                flying[u] = copy
+            elif u < 2:
+                for dim, p in enumerate(partners):
+                    pl.semaphore_signal(free.at[u, dim], inc=1, device_id={"dp": p}, device_id_type=MESH)
+                for copy in waits.pop(u):
+                    copy.wait_send()
+
+    def product(j):
+        load_rhs(j).wait()
+        if j + 1 < 15:
+            load_rhs(j + 1).start()
+        if j in (0, 5):
+            load_lhs(1 if j == 0 else 0).wait()
+        if j % 5 >= 2:
+            store(j - 2).wait()
+
+        def rows(i, _):
+            left = lhs[pl.ds(pl.multiple_of(i * 256, 256), 256), :]
+            out = jnp.dot(left, rhs[j % 2], preferred_element_type=F32).astype(BF16)
+            tile[j % 2, lax.div(i, 2), lax.rem(i, 2)] = out.reshape(2, 2, 2, 32, WIDE)
+            return 0
+
+        lax.fori_loop(0, 4, rows, 0)
+        store(j).start()
+        if j == 4:
+            load_lhs(0).start()
+        if j % 5 == 4:
+            store(j - 1).wait()
+            store(j).wait()
+
+    for t in range(11):
+        steps = [(u, t - ROUND[u]) for u in reversed(range(n)) if 0 <= t - ROUND[u] <= 4]
+        tiles = list(TILES.get(t, ()))
+        while steps or tiles:
+            if steps:
+                step(*steps.pop(0))
+            for _ in range(max(1, -(-len(tiles) // (len(steps) + 1)))):
+                if tiles:
+                    product(tiles.pop(0))
+        if t in (0, 4, 5):
+            begin({0: 1, 4: 4, 5: 5}[t])
+    for u in (2, 3):
+        copy = flying[u]
+        copy.wait_recv()
+        waits[u].append(copy)
+        outs[u][...] = lasts[u][...]
+    for u in waits:
+        for copy in waits[u]:
+            copy.wait_send()
+
+
+def reduce_scatter(given, lefts, rights):
     blocks = lambda shape: pltpu.VMEM((2, 2, 2, 2, *shape), BF16)
-    scratch = [blocks(half_of(k)) for k in kinds] * 2
-    for k in kinds:
+    scratch = [blocks(half_of(k)) for k in SLOT_KINDS] * 2
+    for k in SLOT_KINDS:
         for color in range(3):
             for s in range(4):
                 scratch.append(pltpu.VMEM((2,) * (3 - s) + part_of(k, color)[1], BF16))
-    scratch += [pltpu.VMEM((200, 1024), BF16)] * kinds.count("d")
-    scratch += [pltpu.SemaphoreType.DMA((n, 14)), pltpu.SemaphoreType.DMA((n, 14)), pltpu.SemaphoreType.DMA((n,))]
+    scratch += [pltpu.VMEM((200, 1024), BF16)] * 2
+    scratch += [pltpu.VMEM((1024, 2048), BF16), pltpu.VMEM((2, 2048, WIDE), BF16), pltpu.VMEM((2, 2, 2, 2, 2, 2, 32, WIDE), BF16)]
+    dma = pltpu.SemaphoreType.DMA
+    scratch += [dma((6, 14)), dma((6, 14)), dma((6,)), pltpu.SemaphoreType.REGULAR((2, 5)), dma, dma((2,)), dma((2,))]
+    hbm, vmem = pl.BlockSpec(memory_space=pltpu.HBM), pl.BlockSpec(memory_space=pltpu.VMEM)
+    sums = [jax.ShapeDtypeStruct((200, 1024) if k == "d" else (32, 3200), BF16) for k, _ in REDUCED]
+    products = [jax.ShapeDtypeStruct((2, 2, 2, 2, 2, 32, 3200), BF16)] * 3
     return pl.pallas_call(
-        functools.partial(reduce_kernel, kinds),
-        out_shape=[jax.ShapeDtypeStruct((200, 1024) if k == "d" else (32, 3200), BF16) for k in kinds],
-        in_specs=[pl.BlockSpec(memory_space=pltpu.HBM)] * n,
-        out_specs=[pl.BlockSpec(memory_space=pltpu.VMEM)] * n,
+        reduce_kernel,
+        out_shape=sums + products,
+        in_specs=[hbm] * 8,
+        out_specs=[vmem] * 6 + [hbm] * 3,
         scratch_shapes=scratch,
-        compiler_params=pltpu.CompilerParams(collective_id=collective_id, has_side_effects=True, vmem_limit_bytes=62 * 2**20),
-        name=f"reduce_{collective_id}",
-    )(*grads)
+        compiler_params=pltpu.CompilerParams(collective_id=0, has_side_effects=True, vmem_limit_bytes=63 * 2**20),
+        name="reduce",
+    )(*given, *lefts, *rights)[:6]
 
 
 def gather_kernel(kinds, *refs):
@@ -314,31 +391,28 @@
 
         d = dy
         grads, new, full = {}, {}, {}
+        lefts, rights = {}, {}
         for i in reversed(range(layers)):
             h, a, scale, gate, up, act = saved[i]
             d_act = dot(d, wd[i], 1, 1).astype(BF16).astype(F32)
             sig = jax.nn.sigmoid(gate)
             d_up = (d_act * (gate * sig)).astype(BF16)
             d_gate = (d_act * up * (sig * (1 + gate * (1 - sig)))).astype(BF16)
-            grads["g", i] = dot(a, d_gate, 0, 0).astype(BF16)
+            lefts[i] = a.T
+            rights["g", i], rights["u", i] = d_gate, d_up
             if i:
-                early = lax.psum_scatter(grads.pop(("g", i)).reshape(32, 32, 3200), "dp", scatter_dimension=0, tiled=True)
+                grads["g", i] = dot(a, d_gate, 0, 0).astype(BF16)
             grads["d", i] = dot(act, d, 0, 0).astype(BF16)
-            if not i:
-                early, grads["g", 0], grads["d", 0] = lax.optimization_barrier((early, grads["g", 0], grads["d", 0]))
-                new["g", 1] = update("g", 1, early[0])
-                block, d_up = lax.optimization_barrier((new["g", 1][0], d_up))
-                full["g", 1] = lax.all_gather(block, "dp", axis=0, tiled=True)
-            grads["u", i] = dot(a, d_up, 0, 0).astype(BF16)
             if i:
                 da = dot(d_gate, wg[i], 1, 1).astype(BF16) + dot(d_up, wu[i], 1, 1).astype(BF16)
                 da = da.astype(F32)
                 wide = h.astype(F32)
                 inner = jnp.mean(da * wide, -1, keepdims=True)
                 d = d + (scale * da - wide * (scale**3 * inner)).astype(BF16)
-        units = [("u", 1), ("d", 1), ("g", 0), ("u", 0), ("d", 0)]
+        units = REDUCED
         kinds = tuple(k for k, _ in units)
-        summed = dict(zip(units, reduce_scatter([by_chips(grads[u], u[0]) for u in units], kinds, 0)))
+        given = [by_chips(grads[u], u[0]) for u in (units[0], units[2], units[3])]
+        summed = dict(zip(units, reduce_scatter(given, [lefts[0], lefts[1]], [rights[units[u]] for u in COMPUTED])))
         for kind, i in units:
             g = summed[kind, i]
             if kind == "d":

time: 794 us -> 765 us (0.963)
  matrix products: 361 us -> 299 us
  Pallas kernels: 310 us -> 356 us
  between operations: 14.8 us -> 1.36 us
    dot_general x15 -> x12, matrix products: 361 us -> 299 us  [dot(): lax.dot_general(a, b, (((ca,), (cb,)), ((), ())), preferred_element_type=...]
    pallas_call x1, Pallas kernels: 160 us -> 184 us  [reduce_scatter(): pl.pallas_call(reduce_kernel, out_shape=sums + products, in_specs=[hbm] *...]
    pallas_call x1, Pallas kernels: 150 us -> 172 us  [all_gather(): pl.pallas_call(functools.partial(gather_kernel, kinds), out_shape=[jax.Sh...]
    transpose x0 -> x2, other arithmetic: none -> 9.88 us  [local(): lefts[i] = a.T]
    unnamed x52 -> x54, local copies, waits for them, and re-layouts: 17.8 us -> 18.5 us
  transfers between devices with their start and end apart: 3 -> 1, of which waited for: 0 -> 0; matrix products, arithmetic and copies ran while one was open for 33% -> 4% of each run, Pallas kernels for 39% -> 0%
where the time goes in v3:
time: 765 us; the launch traced here: 758 us
  Pallas kernels  356 us (47%)
  matrix products  299 us (39%)
  other arithmetic  52.4 us (7%)
  local copies, waits for them, and re-layouts  49.3 us (6%)
    dot_general x12, matrix products, dot(): lax.dot_general(a, b, (((ca,), (cb,)), ((), ())), preferred_element_type=...  299 us
    pallas_call x1, Pallas kernels, reduce_scatter(): pl.pallas_call(reduce_kernel, out_shape=sums + products, in_specs=[hbm] *...  184 us
    pallas_call x1, Pallas kernels, all_gather(): pl.pallas_call(functools.partial(gather_kernel, kinds), out_shape=[jax.Sh...  172 us
    another operation x3, other arithmetic, local(): outs = [jnp.stack([full[k, i] for i in range(layers)]) for k in 'gud']  25.3 us
    unnamed x54, local copies, waits for them, and re-layouts  18.5 us
  transfers between devices with their start and end apart: 1, of which 0 were waited for; matrix products, arithmetic and copies ran while one was open for 4% of the time, Pallas kernels for 0%

profile of v3, /device:TPU:0, one launch (start us, length us, event | category | flops | bytes accessed | tf_op | source)
XLA Modules:
  0.0 757.8 jit_solution(5860493765904975541)
XLA Ops:
  0.6 6.5 copy.20
  7.2 3.1 fusion.9
  10.2 0.0 copy-start.13
  10.2 21.9 %fusion.31 = f32[2048,3200]{1,0:T(8,128)} fusion(bf16[1,2048,1024]{2,1,0:T(8,128)(2,1)} %param.11, f32[2048]{0:T(1024)S(1)} %add_rsqrt_fusion.1, bf16[2,1024,3200]{2,1,0:T(8,128)(2,1)} %param.13), kind=kOutput, calls=%fused_computation.54 | convolution fusion | flops 13428064256 | bytes 36970496 | tf_op jit(solution)/shard_map/dot_general | solution.py:23
  32.1 0.0 copy-done.13
  32.1 32.1 %multiply_convert_fusion.1 = (bf16[2048,3200]{1,0:T(8,128)(2,1)}, f32[2048,3200]{1,0:T(8,128)}) fusion(f32[2048,3200]{1,0:T(8,128)} %fusion.31, bf16[2,1024,3200]{2,1,0:T(8,128)(2,1)} %param.14, bf16[1,2048,1024]{2,1,0:T(8,128)(2,1)} %param.11, f32[2048]{0:T(1024)S(1)} %add_rsqrt_fusion.1), kind=kOutput, calls=%fused_computation.13 | convolution fusion | flops 13467385856 | bytes 76292096 | tf_op jit(solution)/shard_map/dot_general | solution.py:23
  64.2 22.1 %fusion.13 = (f32[2048]{0:T(1024)S(1)}, bf16[2048,1024]{0,1:T(8,128)(2,1)}) fusion(bf16[2048,3200]{1,0:T(8,128)(2,1)} %get-tuple-element.80, bf16[2,3200,1024]{2,1,0:T(8,128)(2,1)} %param.15, bf16[1,2048,1024]{1,2,0:T(8,128)(2,1)} %copy.20), kind=kOutput, calls=%fused_computation.33 | convolution fusion | flops 13432256512 | bytes 28057600 | tf_op jit(solution)/shard_map/dot_general | solution.py:23
  86.3 0.6 copy-done.15
  86.9 23.4 %fusion.19 = f32[2048,3200]{1,0:T(8,128)} fusion(bf16[2048,1024]{0,1:T(8,128)(2,1)} %get-tuple-element.83, f32[2048]{0:T(1024)S(1)} %add_rsqrt_fusion, bf16[2,1024,3200]{2,1,0:T(8,128)(2,1)} %param.13), kind=kOutput, calls=%fused_computation.42 | convolution fusion | flops 13428064256 | bytes 36970496 | tf_op jit(solution)/shard_map/dot_general | solution.py:23
  110.3 0.0 copy-done
  110.3 20.9 %fusion.23 = f32[2048,3200]{1,0:T(8,128)} fusion(bf16[2048,1024]{0,1:T(8,128)(2,1)S(1)} %copy-done, f32[2048]{0:T(1024)S(1)} %add_rsqrt_fusion, bf16[2,1024,3200]{2,1,0:T(8,128)(2,1)} %param.14), kind=kOutput, calls=%fused_computation.46 | convolution fusion | flops 13428064256 | bytes 36970496 | tf_op jit(solution)/shard_map/dot_general | solution.py:23
  131.2 0.0 copy-done.7
  131.2 35.0 %fusion.2 = (bf16[2048,3200]{1,0:T(8,128)(2,1)}, bf16[2048,3200]{1,0:T(8,128)(2,1)}) fusion(f32[2048,3200]{1,0:T(8,128)} %fusion.19, f32[2048,3200]{1,0:T(8,128)} %fusion.23, bf16[2,3200,1024]{2,1,0:T(8,128)(2,1)} %param.15, bf16[1,2048,1024]{2,1,0:T(8,128)(2,1)S(1)} %copy-done.7), kind=kOutput, calls=%fused_computation.6 | convolution fusion | flops 13520076800 | bytes 89391104 | tf_op jit(solution)/shard_map/dot_general | solution.py:23
  166.2 25.7 %fusion.16 = bf16[3200,1024]{1,0:T(8,128)(2,1)} fusion(f32[2048,3200]{1,0:T(8,128)} %fusion.23, f32[2048,3200]{1,0:T(8,128)} %fusion.19, bf16[1,2048,1024]{2,1,0:T(8,128)(2,1)} %param.12), kind=kOutput, calls=%fused_computation.37 | convolution fusion | flops 13464371200 | bytes 63176704 | tf_op jit(solution)/shard_map/dot_general | solution.py:23
  191.9 21.2 %convolution_convert_fusion.3 = bf16[1024,3200]{1,0:T(8,128)(2,1)} fusion(bf16[2048,3200]{1,0:T(8,128)(2,1)} %get-tuple-element.45, bf16[2048,1024]{0,1:T(8,128)(2,1)} %get-tuple-element.83, f32[2048]{0:T(1024)S(1)} %add_rsqrt_fusion), kind=kOutput, calls=%fused_computation.39 | convolution fusion | flops 13431341056 | bytes 23863296 | tf_op jit(solution)/shard_map/dot_general | solution.py:23
  213.1 0.0 copy-done.3
  213.1 18.0 %fusion.17 = bf16[2048,1024]{0,1:T(8,128)(2,1)} fusion(bf16[2048,3200]{1,0:T(8,128)(2,1)} %get-tuple-element.45, bf16[2,1024,3200]{2,1,0:T(8,128)(2,1)S(1)} %copy-done.3), kind=kOutput, calls=%fused_computation.40 | convolution fusion | flops 13421772800 | bytes 23855104 | tf_op jit(solution)/shard_map/dot_general | solution.py:23
  231.1 6.4 copy.21
  237.6 5.5 fusion.36.refs_3_
  243.1 10.7 %fusion.111 = (bf16[1,3200,1024]{2,1,0:T(8,128)(2,1)}, bf16[1,3200,1024]{2,1,0:T(8,128)(2,1)}) fusion(bf16[2,3200,1024]{2,1,0:T(8,128)(2,1)} %param.15), kind=kLoop, calls=%fused_computation.170 | loop fusion | bytes 26214400 | tf_op jit(solution)/shard_map/slice | solution.py:380
  253.8 19.2 %convert_add_fusion = bf16[2048,1024]{0,1:T(8,128)(2,1)S(1)} fusion(bf16[2048,1024]{0,1:T(8,128)(2,1)} %fusion.17, bf16[2048,3200]{1,0:T(8,128)(2,1)} %get-tuple-element.44.refs_5_, bf16[2,1024,3200]{2,1,0:T(8,128)(2,1)} %param.14), kind=kOutput, calls=%fused_computation.62 | convolution fusion | flops 13425967104 | bytes 28049408 | tf_op jit(solution)/shard_map/dot_general | solution.py:23
  273.0 0.0 copy-start.16
  273.0 0.0 copy-start.2
  273.0 4.4 fusion.43
  277.4 0.0 copy-done.16
  277.4 3.2 fusion.35
  280.6 20.7 %convolution_convert_fusion.2 = bf16[3200,1024]{1,0:T(8,128)(2,1)} fusion(bf16[2048,3200]{1,0:T(8,128)(2,1)} %get-tuple-element.80, bf16[2048,1024]{0,1:T(8,128)(2,1)S(1)} %fusion.35), kind=kOutput, calls=%fused_computation.38 | convolution fusion | flops 13425049600 | bytes 23855104 | tf_op jit(solution)/shard_map/dot_general | solution.py:23
  301.4 38.6 %fusion.5 = (bf16[2048,3200]{1,0:T(8,128)(2,1)}, bf16[2048,3200]{1,0:T(8,128)(2,1)}) fusion(f32[2048,3200]{1,0:T(8,128)} %fusion.31, f32[2048,3200]{1,0:T(8,128)} %get-tuple-element.81, bf16[2048,1024]{0,1:T(8,128)(2,1)} %copy-done.6, bf16[2,3200,1024]{2,1,0:T(8,128)(2,1)} %param.15), kind=kOutput, calls=%fused_computation.9 | convolution fusion | flops 13520076800 | bytes 89391104 | tf_op jit(solution)/shard_map/dot_general | solution.py:23
  340.0 0.6 fusion.113
  340.6 0.0 copy-done.12
  340.6 1.5 fusion.112
  342.2 183.7 %reduce.1 = (bf16[32,3200]{1,0:T(8,128)(2,1)}, bf16[32,3200]{1,0:T(8,128)(2,1)}, bf16[200,1024]{1,0:T(8,128)(2,1)}, bf16[200,1024]{1,0:T(8,128)(2,1)}, bf16[32,3...) custom-call(bf16[2,2,2,2,2,32,3200]{6,5,4,3,2,1,0:T(8,128)(2,1)} %bi, ...), custom_call_target="tpu_custom_call" | custom-call | tf_op jit(solution)/shard_map/reduce/pallas_call | solution.py:274
  525.9 2.1 fusion.86
  528.0 0.0 slice-start
  528.0 0.8 pad_maximum_fusion.9
  528.9 0.0 collective-permute-start
  528.9 11.8 %fusion.110 = (bf16[1,1024,3200]{2,1,0:T(8,128)(2,1)}, bf16[1,1024,3200]{2,1,0:T(8,128)(2,1)}) fusion(bf16[2,1024,3200]{2,1,0:T(8,128)(2,1)} %param.13), kind=kLoop, calls=%fused_computation.169 | loop fusion | bytes 26214400 | tf_op jit(solution)/shard_map/slice | solution.py:375
  540.7 0.0 slice-done.1
  540.7 0.0 copy-start.8
  540.7 5.4 fusion.109
  546.1 0.1 pad_maximum_fusion.3
  546.2 0.0 copy-start.9
  546.2 1.5 copy.26
  547.7 0.1 pad_maximum_fusion.4
  547.8 0.0 copy-start.10
  547.8 1.5 copy.27
  549.3 2.6 fusion.75
  552.0 1.3 pad_maximum_fusion.5
  553.3 0.0 copy-done.10
  553.3 2.4 fusion.78
  555.7 1.3 pad_maximum_fusion.6
  557.0 0.0 collective-permute-done
  557.0 0.1 broadcast_select_fusion
  557.0 0.2 fusion.83
  557.2 0.8 slice_bitcast_fusion
  558.0 172.2 %gather_1.1 = (bf16[2,2,2,2,2,32,3200]{6,5,4,3,2,1,0:T(8,128)(2,1)}, bf16[2,2,2,2,2,32,3200]{6,5,4,3,2,1,0:T(8,128)(2,1)}, bf16[2,2,2,2,200,1024]{5,4,3,2,1,0:T(...) custom-call(bf16[32,3200]{1,0:T(8,128)(2,1)} %get-tuple-element.57.r, ...), custom_call_target="tpu_custom_call" | custom-call | tf_op jit(solution)/shard_map/gather_1/pallas_call | solution.py:352
  730.2 0.0 slice-start.4
  730.2 0.0 slice-start.6
  730.2 12.7 %pad_maximum_fusion = bf16[2,1024,3200]{2,1,0:T(8,128)(2,1)} fusion(bf16[1,1024,3200]{2,1,0:T(8,128)(2,1)} %bitcast.231, bf16[1,1024,3200]{2,1,0:T(8,128)(2,1)} %bitcast.232), kind=kLoop, calls=%fused_computation.23 | loop fusion | flops 6553600 | bytes 26214400 | tf_op jit(solution)/shard_map/stack | solution.py:429
  742.9 0.7 copy-done.5
  743.6 7.3 pad_maximum_fusion.1
  750.9 0.0 slice-done.5
  750.9 1.1 slice-done.7
  752.0 5.3 pad_maximum_fusion.2
  (35 shorter events, 0.1 us)
Async XLA Ops:
  10.2 21.9 %copy-start.13 = (f32[2048]{0:T(1024)}, f32[2048]{0:T(1024)S(1)}, u32[]{:S(2)}) copy-start(f32[2048]{0:T(1024)S(1)} %add_rsqrt_fusion.1) | copy-start | bytes 24580
  86.3 0.6 copy-start.15
  86.9 23.4 %copy-start = (bf16[2048,1024]{0,1:T(8,128)(2,1)S(1)}, bf16[2048,1024]{0,1:T(8,128)(2,1)}, u32[]{:S(2)}) copy-start(bf16[2048,1024]{0,1:T(8,128)(2,1)} %get-tuple-element.83) | copy-start | bytes 12582916
  110.3 20.9 %copy-start.7 = (bf16[1,2048,1024]{2,1,0:T(8,128)(2,1)S(1)}, bf16[1,2048,1024]{2,1,0:T(8,128)(2,1)}, u32[]{:S(2)}) copy-start(bf16[1,2048,1024]{2,1,0:T(8,128)(2,1)} %param.12) | copy-start | bytes 12582916
  191.9 21.2 %copy-start.3 = (bf16[2,1024,3200]{2,1,0:T(8,128)(2,1)S(1)}, bf16[2,1024,3200]{2,1,0:T(8,128)(2,1)}, u32[]{:S(2)}) copy-start(bf16[2,1024,3200]{2,1,0:T(8,128)(2,1)} %param.13) | copy-start | bytes 39321604
  231.1 6.4 copy-start.14
  253.8 19.2 %copy-start.1 = (bf16[2048,1024]{0,1:T(8,128)(2,1)S(1)}, bf16[2048,1024]{0,1:T(8,128)(2,1)}, u32[]{:S(2)}) copy-start(bf16[2048,1024]{0,1:T(8,128)(2,1)} %get-tuple-element.83) | copy-start | bytes 12582916
  273.0 4.4 copy-start.16
  273.0 4.4 copy-start.2
  280.6 20.8 %copy-start.6 = (bf16[2048,1024]{0,1:T(8,128)(2,1)}, bf16[2048,1024]{0,1:T(8,128)(2,1)S(1)}, u32[]{:S(2)}) copy-start(bf16[2048,1024]{0,1:T(8,128)(2,1)S(1)} %fusion.35) | copy-start | bytes 12582916
  301.4 38.6 %copy-start.11 = (f32[2,100,1024]{2,0,1:T(2,128)S(1)}, f32[2,100,1024]{2,0,1:T(2,128)}, u32[]{:S(2)}) copy-start(f32[2,100,1024]{2,0,1:T(2,128)} %param.21) | copy-start | bytes 2457604
  301.4 39.2 %copy-start.12 = (f32[2,100,1024]{2,0,1:T(2,128)S(1)}, f32[2,100,1024]{2,0,1:T(2,128)}, u32[]{:S(2)}) copy-start(f32[2,100,1024]{2,0,1:T(2,128)} %param.18) | copy-start | bytes 2457604
  528.0 12.7 %slice-start = ((s8[13107200]{0:T(1024)(128)(4,1)}), s8[4194304]{0:T(1024)(128)(4,1)S(1)}, s32[]{:S(2)}) async-start(s8[13107200]{0:T(1024)(128)(4,1)} %bitcast.218), calls=%async_computation | async-start | bytes 8388608
  528.9 11.8 %slice-start.1 = ((s8[13107200]{0:T(1024)(128)(4,1)}), s8[4194304]{0:T(1024)(128)(4,1)S(1)}, s32[]{:S(2)}) async-start(s8[13107200]{0:T(1024)(128)(4,1)} %bitcast.218), calls=%async_computation.1 | async-start | bytes 8388608
  528.9 11.9 %slice-start.2 = ((s8[13107200]{0:T(1024)(128)(4,1)}), s8[4194304]{0:T(1024)(128)(4,1)S(1)}, s32[]{:S(2)}) async-start(s8[13107200]{0:T(1024)(128)(4,1)} %bitcast.218), calls=%async_computation.2 | async-start | bytes 8388608
  528.9 11.9 %slice-start.3 = ((s8[13107200]{0:T(1024)(128)(4,1)}), s8[524288]{0:T(1024)(128)(4,1)S(1)}, s32[]{:S(2)}) async-start(s8[13107200]{0:T(1024)(128)(4,1)} %bitcast.218), calls=%async_computation.3 | async-start | bytes 1048576
  528.9 28.1 %collective-permute-start = (bf16[2,100,1024]{2,1,0:T(8,128)(2,1)}, bf16[2,100,1024]{2,1,0:T(8,128)(2,1)S(1)}, u32[]{:S(2)}, u32[]{:S(2)}) collective-permute-start(bf16[2,100,1024]{2,1,0:T(8,128)(2,1)} %pad_maximum_fusion.9), channel_id=1, source_target_pairs={{0,1},{1,0},{2,3},{3,2},{4,5},{5,4},{6,7},{7,6},{8,9},{9,8},{10,11... | collective-permute-start | bytes 1228808 | tf_op jit(solution)/shard_map/ppermute | solution.py:422
  540.7 8.6 %copy-start.8 = (f32[2,32,3200]{2,1,0:T(8,128)S(1)}, f32[2,32,3200]{2,1,0:T(8,128)}, u32[]{:S(2)}) copy-start(f32[2,32,3200]{2,1,0:T(8,128)} %param.16) | copy-start | bytes 2457604
  546.2 7.1 copy-start.9
  547.8 5.5 copy-start.10
  730.2 12.7 %copy-start.4 = (bf16[2,2,2,2,2,32,3200]{6,5,4,3,2,1,0:T(8,128)(2,1)S(1)}, bf16[2,2,2,2,2,32,3200]{6,5,4,3,2,1,0:T(8,128)(2,1)}, u32[]{:S(2)}) copy-start(bf16[2,2,2,2,2,32,3200]{6,5,4,3,2,1,0:T(8,128)(2,1)} %get-tuple-element.30) | copy-start | bytes 19660804
  730.2 13.4 %copy-start.5 = (bf16[2,2,2,2,2,32,3200]{6,5,4,3,2,1,0:T(8,128)(2,1)S(1)}, bf16[2,2,2,2,2,32,3200]{6,5,4,3,2,1,0:T(8,128)(2,1)}, u32[]{:S(2)}) copy-start(bf16[2,2,2,2,2,32,3200]{6,5,4,3,2,1,0:T(8,128)(2,1)} %get-tuple-element.29) | copy-start | bytes 19660804
  730.2 20.7 %slice-start.4 = ((s8[6553600]{0:T(1024)(128)(4,1)}), s8[4194304]{0:T(1024)(128)(4,1)S(1)}, s32[]{:S(2)}) async-start(s8[6553600]{0:T(1024)(128)(4,1)} %bitcast.223), calls=%async_computation.4 | async-start | bytes 8388608
  730.2 20.7 %slice-start.6 = ((s8[6553600]{0:T(1024)(128)(4,1)}), s8[4194304]{0:T(1024)(128)(4,1)S(1)}, s32[]{:S(2)}) async-start(s8[6553600]{0:T(1024)(128)(4,1)} %bitcast.226), calls=%async_computation.6 | async-start | bytes 8388608
  743.6 7.3 slice-start.5
  743.6 8.4 %slice-start.7 = ((s8[6553600]{0:T(1024)(128)(4,1)}), s8[2359296]{0:T(1024)(128)(4,1)S(1)}, s32[]{:S(2)}) async-start(s8[6553600]{0:T(1024)(128)(4,1)} %bitcast.226), calls=%async_computation.7 | async-start | bytes 4718592

commit v4 on v3

--- a/solution.py
+++ b/solution.py
@@ -13,6 +13,13 @@
 WEIGHT = (16, 8, 4, 2, 1)
 X, Y, Z1, Z0, CORE = range(5)
 ORDERS = ((X, Y, Z0, Z1), (Y, X, Z0, Z1), (Z0, Z1, X, Y))
+
+
+def order_of(unit, color):
+    order = ORDERS[color]
+    return (*order[:2], order[3], order[2]) if color == 2 and unit % 2 else order
+
+
 COLUMNS = ((0, 1280), (1280, 1280), (2560, 640))
 ROWS = ((0, 80), (80, 80), (160, 40))
 ROWWISE, COLWISE = (32, 3200), (200, 512)
@@ -94,7 +101,7 @@
 SLOT_KINDS = ("g", "u", "d", "d")
 COMPUTED = (1, 4, 5)
 WIDE = 640
-TILES = {0: range(0, 5), 1: range(5, 7), 2: range(7, 9), 3: range(9, 11), 4: range(11, 13), 5: range(13, 15)}
+TILES = {0: range(0, 5), 1: range(5, 8), 2: range(8, 10), 3: range(10, 12), 4: range(12, 15)}
 
 
 def reduce_kernel(*refs):
@@ -157,13 +164,13 @@
         where = (*at, *part_of(kinds[u], color)[0])
         value = totals[SLOT[u]][where].astype(F32) + firsts[SLOT[u]][where].astype(F32)
         for s in range(steps):
-            rest = tuple(at[i] for i in range(4) if i not in ORDERS[color][: s + 1])
+            rest = tuple(at[i] for i in range(4) if i not in order_of(u, color)[: s + 1])
             got = gots[SLOT[u]][color * 4 + s]
             value += (got[rest] if rest else got[...]).astype(F32)
         return value.astype(BF16)
 
     def launch(u, color, s):
-        dim = ORDERS[color][s]
+        dim = order_of(u, color)[s]
         part, _ = part_of(kinds[u], color)
         index = list(state[u, color])
         index[dim] = 1 - bits[dim]
@@ -238,15 +245,22 @@
 
     for t in range(11):
         steps = [(u, t - ROUND[u]) for u in reversed(range(n)) if 0 <= t - ROUND[u] <= 4]
+        if t in (4, 5):
+            steps.remove((t - 4, 4))
+            steps.insert(t - 4, (t - 4, 4))
         tiles = list(TILES.get(t, ()))
+        taken = 0
         while steps or tiles:
             if steps:
                 step(*steps.pop(0))
+                taken += 1
+            if t in (4, 5) and taken == t - 2 and t not in started:
+                begin(t)
             for _ in range(max(1, -(-len(tiles) // (len(steps) + 1)))):
                 if tiles:
                     product(tiles.pop(0))
-        if t in (0, 4, 5):
-            begin({0: 1, 4: 4, 5: 5}[t])
+        if t == 0:
+            begin(1)
     for u in (2, 3):
         copy = flying[u]
         copy.wait_recv()
@@ -307,7 +321,7 @@
         sent.append((copy, True))
 
     def launch(u, color, s, src=None):
-        dim = ORDERS[color][3 - s]
+        dim = order_of(u, color)[3 - s]
         dst = at(u, state[u, color], color)
         copy = remote(dst if src is None else src, dst, send.at[u, 9 * color + s], recv.at[u, 9 * color + s], partners[dim])
         copy.start()
@@ -333,7 +347,7 @@
                     sent.append((copy, False))
                     if s == 1:
                         flying["own", u, color].wait()
-                    dim = ORDERS[color][4 - s]
+                    dim = order_of(u, color)[4 - s]
                     fresh = list(state[u, color])
                     fresh[dim] = 1 - bits[dim]
                     state[u, color][dim] = None
@@ -378,14 +392,6 @@
             saved.append((h, a, scale, gate, up, act))
             if i + 1 < layers:
                 h = h + dot(act, wd[i], 1, 0).astype(BF16)
-        def rows_of(t, kind):
-            rows = old[kind][1].shape[1]
-            return lax.dynamic_slice_in_dim(t, me * rows, rows, 0)
-
-        def update(kind, i, g):
-            w, m, v = (t[i] for t in old[kind])
-            return adamw(rows_of(w, kind).astype(F32), m, v, g.astype(F32))
-
         def by_chips(t, kind):
             return t.reshape(2, 2, 2, 2, 200, 1024) if kind == "d" else t.reshape(2, 2, 2, 2, 2, 32, 3200)
 
@@ -413,22 +419,25 @@
         kinds = tuple(k for k, _ in units)
         given = [by_chips(grads[u], u[0]) for u in (units[0], units[2], units[3])]
         summed = dict(zip(units, reduce_scatter(given, [lefts[0], lefts[1]], [rights[units[u]] for u in COMPUTED])))
-        for kind, i in units:
-            g = summed[kind, i]
+        for kind in KINDS:
+            w, m, v = old[kind]
+            rows = m.shape[1]
+            g = jnp.stack([summed[kind, i] for i in range(layers)])
             if kind == "d":
-                g = lax.dynamic_slice_in_dim(g, core * 100, 100, 0)
-            new[kind, i] = update(kind, i, g)
-        mine = jnp.stack([new["d", i][0] for i in range(layers)])
+                g = lax.dynamic_slice_in_dim(g, core * rows, rows, 1)
+            mine = lax.dynamic_slice_in_dim(w, me * rows, rows, 1)
+            new[kind] = adamw(mine.astype(F32), m, v, g.astype(F32))
+        mine = new["d"][0]
         other = lax.ppermute(mine, "dp", [(k, k + 1 - 2 * (k % 2)) for k in range(32)])
         first = core == 0
         whole = jnp.concatenate([jnp.where(first, mine, other), jnp.where(first, other, mine)], 1)
         part = lax.dynamic_slice_in_dim(whole, core * 512, 512, 2)
-        blocks = [part[i] if kind == "d" else new[kind, i][0] for kind, i in units]
+        blocks = [part[i] if kind == "d" else new[kind][0][i] for kind, i in units]
         for (kind, i), t in zip(units, all_gather(blocks, kinds, 1)):
             full[kind, i] = t.reshape(old[kind][0].shape[1:])
         outs = [jnp.stack([full[k, i] for i in range(layers)]) for k in "gud"]
         for which in (1, 2):
-            outs += [jnp.stack([new[k, i][which] for i in range(layers)]) for k in "gud"]
+            outs += [new[k][which] for k in "gud"]
         return tuple(outs)
 
     seq, whole, rows = P(("rep", "dp")), P(), P(None, "dp")

time: 765 us -> 742 us (0.970)
  local copies, waits for them, and re-layouts: 49.3 us -> 20.2 us
  Pallas kernels: 356 us -> 366 us
    slice x5 -> x0, local copies, waits for them, and re-layouts: 30 us -> none  [the longest x1 11.8 us: local(): gate = dot(a, wg[i], 1, 0)]
    pallas_call x1, Pallas kernels: 184 us -> 197 us  [reduce_scatter(): pl.pallas_call(reduce_kernel, out_shape=sums + products, in_specs=[hbm] *...]
    unnamed x54 -> x40, local copies, waits for them, and re-layouts: 18.5 us -> 17.9 us
  transfers between devices with their start and end apart: 1 -> 1, of which waited for: 0 -> 0; matrix products, arithmetic and copies ran while one was open for 4% -> 1% of each run, Pallas kernels for 0% -> 0%
where the time goes in v4:
time: 742 us; the launch traced here: 735 us
  Pallas kernels  366 us (49%)
  matrix products  299 us (40%)
  other arithmetic  49.4 us (7%)
  local copies, waits for them, and re-layouts  20.2 us (3%)
    dot_general x12, matrix products, dot(): lax.dot_general(a, b, (((ca,), (cb,)), ((), ())), preferred_element_type=...  299 us
    pallas_call x1, Pallas kernels, reduce_scatter(): pl.pallas_call(reduce_kernel, out_shape=sums + products, in_specs=[hbm] *...  197 us
    pallas_call x1, Pallas kernels, all_gather(): pl.pallas_call(functools.partial(gather_kernel, kinds), out_shape=[jax.Sh...  169 us
    another operation x3, other arithmetic, local(): outs = [jnp.stack([full[k, i] for i in range(layers)]) for k in 'gud']  25.3 us
    unnamed x40, local copies, waits for them, and re-layouts  17.9 us
  transfers between devices with their start and end apart: 1, of which 0 were waited for; matrix products, arithmetic and copies ran while one was open for 1% of the time, Pallas kernels for 0%

profile of v4, /device:TPU:0, one launch (start us, length us, event | category | flops | bytes accessed | tf_op | source)
XLA Modules:
  0.0 735.0 jit_solution(3648189584285843536)
XLA Ops:
  0.6 6.4 copy.20
  7.1 0.0 copy-start.7
  7.1 3.2 fusion.9
  10.3 5.6 fusion.45.refs_3_
  15.9 0.0 copy-done.7
  15.9 20.9 %fusion.31 = f32[2048,3200]{1,0:T(8,128)} fusion(bf16[2,1024,3200]{2,1,0:T(8,128)(2,1)} %param.13, bf16[1,2048,1024]{2,1,0:T(8,128)(2,1)S(1)} %copy-done.7, f32[2048]{0:T(1024)S(1)} %add_rsqrt_fusion.1), kind=kOutput, calls=%fused_computation.54 | convolution fusion | flops 13428064256 | bytes 36970496 | tf_op jit(solution)/shard_map/dot_general | solution.py:30
  36.8 32.1 %multiply_convert_fusion.1 = (bf16[2048,3200]{1,0:T(8,128)(2,1)}, f32[2048,3200]{1,0:T(8,128)}) fusion(f32[2048,3200]{1,0:T(8,128)} %fusion.31, bf16[2,1024,3200]{2,1,0:T(8,128)(2,1)} %param.14, bf16[1,2048,1024]{2,1,0:T(8,128)(2,1)} %param.11, f32[2048]{0:T(1024)S(1)} %add_rsqrt_fusion.1), kind=kOutput, calls=%fused_computation.13 | convolution fusion | flops 13467385856 | bytes 76292096 | tf_op jit(solution)/shard_map/dot_general | solution.py:30
  68.9 22.0 %fusion.13 = (f32[2048]{0:T(1024)S(1)}, bf16[2048,1024]{0,1:T(8,128)(2,1)}) fusion(bf16[2048,3200]{1,0:T(8,128)(2,1)} %get-tuple-element.65, bf16[2,3200,1024]{2,1,0:T(8,128)(2,1)} %param.15, bf16[1,2048,1024]{1,2,0:T(8,128)(2,1)} %copy.20), kind=kOutput, calls=%fused_computation.33 | convolution fusion | flops 13432256512 | bytes 28057600 | tf_op jit(solution)/shard_map/dot_general | solution.py:30
  90.9 0.0 copy-start.11
  90.9 0.0 copy-start.9
  91.0 0.0 copy-start
  91.0 23.4 %fusion.19 = f32[2048,3200]{1,0:T(8,128)} fusion(bf16[2,1024,3200]{2,1,0:T(8,128)(2,1)} %param.13, bf16[2048,1024]{0,1:T(8,128)(2,1)} %get-tuple-element.68, f32[2048]{0:T(1024)S(1)} %add_rsqrt_fusion), kind=kOutput, calls=%fused_computation.42 | convolution fusion | flops 13428064256 | bytes 36970496 | tf_op jit(solution)/shard_map/dot_general | solution.py:30
  114.4 0.0 copy-done.11
  114.4 0.0 copy-done.9
  114.4 0.0 copy-done
  114.4 20.8 %fusion.23 = f32[2048,3200]{1,0:T(8,128)} fusion(bf16[2,1024,3200]{2,1,0:T(8,128)(2,1)} %param.14, bf16[2048,1024]{0,1:T(8,128)(2,1)S(1)} %copy-done, f32[2048]{0:T(1024)S(1)} %add_rsqrt_fusion), kind=kOutput, calls=%fused_computation.46 | convolution fusion | flops 13428064256 | bytes 36970496 | tf_op jit(solution)/shard_map/dot_general | solution.py:30
  135.2 6.5 copy.21
  141.7 25.9 %fusion.16 = bf16[3200,1024]{1,0:T(8,128)(2,1)} fusion(f32[2048,3200]{1,0:T(8,128)} %fusion.23, f32[2048,3200]{1,0:T(8,128)} %fusion.19, bf16[1,2048,1024]{2,1,0:T(8,128)(2,1)} %param.12), kind=kOutput, calls=%fused_computation.37 | convolution fusion | flops 13464371200 | bytes 63176704 | tf_op jit(solution)/shard_map/dot_general | solution.py:30
  167.6 38.8 %fusion.2 = (bf16[2048,3200]{1,0:T(8,128)(2,1)}, bf16[2048,3200]{1,0:T(8,128)(2,1)}) fusion(f32[2048,3200]{1,0:T(8,128)} %fusion.19, f32[2048,3200]{1,0:T(8,128)} %fusion.23, bf16[2,3200,1024]{2,1,0:T(8,128)(2,1)} %param.15, bf16[1,2048,1024]{2,1,0:T(8,128)(2,1)} %param.12), kind=kOutput, calls=%fused_computation.6 | convolution fusion | flops 13520076800 | bytes 89391104 | tf_op jit(solution)/shard_map/dot_general | solution.py:30
  206.4 0.0 copy-start.13
  206.4 20.1 %fusion.17 = bf16[2048,1024]{0,1:T(8,128)(2,1)} fusion(bf16[2048,3200]{1,0:T(8,128)(2,1)} %get-tuple-element.54, bf16[2,1024,3200]{2,1,0:T(8,128)(2,1)} %param.13), kind=kOutput, calls=%fused_computation.40 | convolution fusion | flops 13421772800 | bytes 23855104 | tf_op jit(solution)/shard_map/dot_general | solution.py:30
  226.5 0.0 copy-done.1
  226.5 0.0 copy-done.10
  226.5 0.0 copy-done.13
  226.5 16.0 %convolution_convert_fusion.3 = bf16[1024,3200]{1,0:T(8,128)(2,1)} fusion(bf16[2048,3200]{1,0:T(8,128)(2,1)S(1)} %copy-done.13, bf16[2048,1024]{0,1:T(8,128)(2,1)S(1)} %copy-done.1, f32[2048]{0:T(1024)S(1)} %copy-done.10), kind=kOutput, calls=%fused_computation.39 | convolution fusion | flops 13431341056 | bytes 23863296 | tf_op jit(solution)/shard_map/dot_general | solution.py:30
  242.6 19.2 %convert_add_fusion = bf16[2048,1024]{0,1:T(8,128)(2,1)S(1)} fusion(bf16[2048,1024]{0,1:T(8,128)(2,1)} %fusion.17, bf16[2048,3200]{1,0:T(8,128)(2,1)} %get-tuple-element.53.refs_5_, bf16[2,1024,3200]{2,1,0:T(8,128)(2,1)} %param.14), kind=kOutput, calls=%fused_computation.71 | convolution fusion | flops 13425967104 | bytes 28049408 | tf_op jit(solution)/shard_map/dot_general | solution.py:30
  261.8 0.0 copy-done.2
  261.8 0.0 copy-start.12
  261.8 0.0 copy-start.3
  261.8 4.4 fusion.52
  266.3 0.0 copy-done.12
  266.3 0.0 copy-done.3
  266.3 3.2 fusion.44
  269.5 0.0 copy-start.6
  269.5 20.7 %convolution_convert_fusion.2 = bf16[3200,1024]{1,0:T(8,128)(2,1)} fusion(bf16[2048,3200]{1,0:T(8,128)(2,1)} %get-tuple-element.65, bf16[2048,1024]{0,1:T(8,128)(2,1)S(1)} %fusion.44), kind=kOutput, calls=%fused_computation.38 | convolution fusion | flops 13425049600 | bytes 23855104 | tf_op jit(solution)/shard_map/dot_general | solution.py:30
  290.2 0.0 copy-done.6
  290.2 38.5 %fusion.5 = (bf16[2048,3200]{1,0:T(8,128)(2,1)}, bf16[2048,3200]{1,0:T(8,128)(2,1)}) fusion(f32[2048,3200]{1,0:T(8,128)} %fusion.31, f32[2048,3200]{1,0:T(8,128)} %get-tuple-element.66, bf16[2048,1024]{0,1:T(8,128)(2,1)} %copy-done.6, bf16[2,3200,1024]{2,1,0:T(8,128)(2,1)} %param.15), kind=kOutput, calls=%fused_computation.9 | convolution fusion | flops 13520076800 | bytes 89391104 | tf_op jit(solution)/shard_map/dot_general | solution.py:30
  328.7 196.7 %reduce.1 = (bf16[32,3200]{1,0:T(8,128)(2,1)}, bf16[32,3200]{1,0:T(8,128)(2,1)}, bf16[200,1024]{1,0:T(8,128)(2,1)}, bf16[200,1024]{1,0:T(8,128)(2,1)}, bf16[32,3...) custom-call(bf16[2,2,2,2,2,32,3200]{6,5,4,3,2,1,0:T(8,128)(2,1)} %bi, ...), custom_call_target="tpu_custom_call" | custom-call | tf_op jit(solution)/shard_map/reduce/pallas_call | solution.py:288
  525.5 2.9 fusion.60
  528.3 0.1 collective-permute-start
  528.4 0.0 copy-done.8
  528.4 4.5 fusion.65
  532.9 0.8 slice_bitcast_fusion.1
  533.7 0.8 slice_bitcast_fusion
  534.4 1.5 copy.25
  536.0 1.5 copy.24
  537.5 0.0 collective-permute-done
  537.5 0.1 broadcast_select_fusion
  537.6 0.2 fusion.74
  537.7 0.8 slice_bitcast_fusion.2
  538.5 168.9 %gather_1.1 = (bf16[2,2,2,2,2,32,3200]{6,5,4,3,2,1,0:T(8,128)(2,1)}, bf16[2,2,2,2,2,32,3200]{6,5,4,3,2,1,0:T(8,128)(2,1)}, bf16[2,2,2,2,200,1024]{5,4,3,2,1,0:T(...) custom-call(bf16[32,3200]{1,0:T(8,128)(2,1)} %get-tuple-element.62.r, ...), custom_call_target="tpu_custom_call" | custom-call | tf_op jit(solution)/shard_map/gather_1/pallas_call | solution.py:366
  707.4 0.0 copy-start.4
  707.4 0.0 copy-start.5
  707.4 0.0 slice-start
  707.4 0.0 slice-start.2
  707.4 12.7 %pad_maximum_fusion = bf16[2,1024,3200]{2,1,0:T(8,128)(2,1)} fusion(bf16[1,1024,3200]{2,1,0:T(8,128)(2,1)} %bitcast.105, bf16[1,1024,3200]{2,1,0:T(8,128)(2,1)} %bitcast.106), kind=kLoop, calls=%fused_computation.23 | loop fusion | flops 6553600 | bytes 26214400 | tf_op jit(solution)/shard_map/stack | solution.py:438
  720.1 0.0 copy-done.4
  720.1 0.7 copy-done.5
  720.8 7.3 pad_maximum_fusion.1
  728.1 0.0 slice-done
  728.1 0.0 slice-done.2
  728.1 0.0 slice-done.1
  728.1 1.1 slice-done.3
  729.2 5.3 pad_maximum_fusion.2
  (11 shorter events, 0.0 us)
Async XLA Ops:
  7.1 8.8 %copy-start.7 = (bf16[1,2048,1024]{2,1,0:T(8,128)(2,1)S(1)}, bf16[1,2048,1024]{2,1,0:T(8,128)(2,1)}, u32[]{:S(2)}) copy-start(bf16[1,2048,1024]{2,1,0:T(8,128)(2,1)} %param.11) | copy-start | bytes 12582916
  90.9 23.5 %copy-start.11 = (f32[2048]{0:T(1024)}, f32[2048]{0:T(1024)S(1)}, u32[]{:S(2)}) copy-start(f32[2048]{0:T(1024)S(1)} %get-tuple-element.67) | copy-start | bytes 24580
  90.9 23.5 %copy-start.9 = (f32[2048]{0:T(1024)}, f32[2048]{0:T(1024)S(1)}, u32[]{:S(2)}) copy-start(f32[2048]{0:T(1024)S(1)} %add_rsqrt_fusion) | copy-start | bytes 24580
  91.0 23.5 %copy-start = (bf16[2048,1024]{0,1:T(8,128)(2,1)S(1)}, bf16[2048,1024]{0,1:T(8,128)(2,1)}, u32[]{:S(2)}) copy-start(bf16[2048,1024]{0,1:T(8,128)(2,1)} %get-tuple-element.68) | copy-start | bytes 12582916
  206.4 20.1 %copy-start.1 = (bf16[2048,1024]{0,1:T(8,128)(2,1)S(1)}, bf16[2048,1024]{0,1:T(8,128)(2,1)}, u32[]{:S(2)}) copy-start(bf16[2048,1024]{0,1:T(8,128)(2,1)} %get-tuple-element.68) | copy-start | bytes 12582916
  206.4 20.1 %copy-start.10 = (f32[2048]{0:T(1024)S(1)}, f32[2048]{0:T(1024)}, u32[]{:S(2)}) copy-start(f32[2048]{0:T(1024)} %copy-done.9) | copy-start | bytes 24580
  206.4 20.1 %copy-start.13 = (bf16[2048,3200]{1,0:T(8,128)(2,1)S(1)}, bf16[2048,3200]{1,0:T(8,128)(2,1)}, u32[]{:S(2)}) copy-start(bf16[2048,3200]{1,0:T(8,128)(2,1)} %get-tuple-element.54) | copy-start | bytes 39321604
  242.6 19.2 %copy-start.2 = (bf16[2048,1024]{0,1:T(8,128)(2,1)S(1)}, bf16[2048,1024]{0,1:T(8,128)(2,1)}, u32[]{:S(2)}) copy-start(bf16[2048,1024]{0,1:T(8,128)(2,1)} %get-tuple-element.68) | copy-start | bytes 12582916
  261.8 4.4 copy-start.12
  261.8 4.5 copy-start.3
  269.5 20.7 %copy-start.6 = (bf16[2048,1024]{0,1:T(8,128)(2,1)}, bf16[2048,1024]{0,1:T(8,128)(2,1)S(1)}, u32[]{:S(2)}) copy-start(bf16[2048,1024]{0,1:T(8,128)(2,1)S(1)} %fusion.44) | copy-start | bytes 12582916
  328.7 199.7 %copy-start.8 = (f32[2,32,3200]{2,1,0:T(8,128)S(1)}, f32[2,32,3200]{2,1,0:T(8,128)}, u32[]{:S(2)}) copy-start(f32[2,32,3200]{2,1,0:T(8,128)} %param.19) | copy-start | bytes 2457604
  528.3 9.2 %collective-permute-start = (bf16[2,100,1024]{2,1,0:T(8,128)(2,1)S(1)}, bf16[2,100,1024]{2,1,0:T(8,128)(2,1)S(1)}, u32[]{:S(2)}, u32[]{:S(2)}) collective-permute-start(bf16[2,100,1024]{2,1,0:T(8,128)(2,1)S(1)} %get-tuple-element.42), channel_id=1, source_target_pairs={{0,1},{1,0},{2,3},{3,2},{4,5},{5,4},{6,7},{7,6},{8,9},{9,8},{10,11... | collective-permute-start | bytes 1228808 | tf_op jit(solution)/shard_map/ppermute | solution.py:431
  707.4 12.7 %copy-start.4 = (bf16[2,2,2,2,2,32,3200]{6,5,4,3,2,1,0:T(8,128)(2,1)S(1)}, bf16[2,2,2,2,2,32,3200]{6,5,4,3,2,1,0:T(8,128)(2,1)}, u32[]{:S(2)}) copy-start(bf16[2,2,2,2,2,32,3200]{6,5,4,3,2,1,0:T(8,128)(2,1)} %get-tuple-element.30) | copy-start | bytes 19660804
  707.4 13.4 %copy-start.5 = (bf16[2,2,2,2,2,32,3200]{6,5,4,3,2,1,0:T(8,128)(2,1)S(1)}, bf16[2,2,2,2,2,32,3200]{6,5,4,3,2,1,0:T(8,128)(2,1)}, u32[]{:S(2)}) copy-start(bf16[2,2,2,2,2,32,3200]{6,5,4,3,2,1,0:T(8,128)(2,1)} %get-tuple-element.29) | copy-start | bytes 19660804
  707.4 20.7 %slice-start = ((s8[6553600]{0:T(1024)(128)(4,1)}), s8[4194304]{0:T(1024)(128)(4,1)S(1)}, s32[]{:S(2)}) async-start(s8[6553600]{0:T(1024)(128)(4,1)} %bitcast.97), calls=%async_computation | async-start | bytes 8388608
  707.4 20.7 %slice-start.2 = ((s8[6553600]{0:T(1024)(128)(4,1)}), s8[4194304]{0:T(1024)(128)(4,1)S(1)}, s32[]{:S(2)}) async-start(s8[6553600]{0:T(1024)(128)(4,1)} %bitcast.100), calls=%async_computation.2 | async-start | bytes 8388608
  720.8 7.3 slice-start.1
  720.8 8.4 %slice-start.3 = ((s8[6553600]{0:T(1024)(128)(4,1)}), s8[2359296]{0:T(1024)(128)(4,1)S(1)}, s32[]{:S(2)}) async-start(s8[6553600]{0:T(1024)(128)(4,1)} %bitcast.100), calls=%async_computation.3 | async-start | bytes 4718592
